TPU v7x, 128 devices: a whole 4x4x4 slice. The times are simulated.
128 devices in a mesh: gx: 8 (over z_hi, y), gz: 16 (over z_lo, x, core).
Axes of the slice: x: 4, y: 4, z: 4 (z_hi: 2, z_lo: 2; z = z_hi * 2 + z_lo), core: 2. Of those that a mesh axis runs over, the one named last changes fastest.
Arguments:
- high_u: bfloat16 [256, 512, 512], P('gx', 'gz'), may hold values from -6 to 6
- high_v: bfloat16 [256, 512, 512], P('gx', 'gz'), may hold values from -6 to 6
- low_u: bfloat16 [2048, 512], P(('gx', 'gz')), may hold values from -0.25 to 0.25
- low_v: bfloat16 [2048, 512], P(('gx', 'gz')), may hold values from -0.25 to 0.25
- low_kx: int32 [2048], P(('gx', 'gz')), may hold values from 0 to 64, as said below
- low_kz: int32 [2048], P(('gx', 'gz')), may hold values from 0 to 64, as said below
- tau_inverse: bfloat16 [2048, 512, 512], P(('gx', 'gz')), may hold values from -0.25 to 0.25
Outputs:
- high_term: bfloat16 [256, 512, 512], P('gx', 'gz')
- low_response: float32 [2048, 512], P(('gx', 'gz'))
Inputs may be any that keep to these rules, and one draw needn't show every extreme that they name: Slot m holds the retained mode (low_kx[m], low_kz[m]); no two slots hold the same pair; the device that holds slot m owns that mode. `low_kz`: paired with low_kx slot by slot.
All inputs are finite; a program needn't handle non-finite values.
Results may differ from a plain program's by a relative error of at most 0.0047.
Values may be sent and summed in bfloat16 or wider, within the bound.
No kernel may reach another device: no remote copies, remote signals or barrier semaphores. Data moves between devices by JAX's collectives and lax.ppermute only.
A program may use at most 128 MiB of HBM per device.

v0:
```python
import functools
import math

import jax
import jax.numpy as jnp
from jax import lax
from jax.experimental import pallas as pl
from jax.experimental.pallas import tpu as pltpu
from jax.sharding import PartitionSpec as P

KL = 32
SIDE = 2 * KL + 1
PADDED = 80
LANES = 128
HALF = LANES // 2
AXES = ("gx", "gz")
INTERPRET = False
VMEM_LIMIT = 48 * 1024 * 1024
bf16 = jnp.bfloat16
f32 = jnp.float32


def axis_table(index, positions, length):
    wavenum = jnp.where(index <= KL, index, index - KL)
    phases = wavenum[:, None] * positions[None, :] % length
    angles = phases.astype(f32) * (2.0 * math.pi / length)
    return jnp.where((index <= KL)[:, None], jnp.cos(angles), jnp.sin(angles))


def split(values):
    top = lax.reduce_precision(values, 8, 7)
    return top.astype(bf16), (values - top).astype(bf16)


def halves(values):
    top = values.astype(bf16)
    return top, (values - top.astype(f32)).astype(bf16)


def dot(a, b):
    return jnp.dot(a, b, preferred_element_type=f32)


def x_tables(groups_x, groups, group, length_x):
    part = jnp.arange(group, dtype=jnp.int32)[:, None, None]
    device = jnp.arange(groups_x, dtype=jnp.int32)[None, :, None]
    block = jnp.arange(groups, dtype=jnp.int32)[None, None, :]
    where_x = (device * (group * groups) + block * group + part).reshape(-1)
    index = jnp.arange(PADDED, dtype=jnp.int32)
    table = axis_table(index, where_x, length_x)
    table = jnp.where((index < SIDE)[:, None], table, 0.0)
    top, rest = split(table)
    forward = jnp.concatenate([top, rest], axis=0)
    top, rest = split(table.T)
    return forward, jnp.concatenate([top, rest], axis=1)


def z_tables(group, cells_z, length_z):
    column = jnp.arange(length_z * group, dtype=jnp.int32)
    where_z = column // (group * cells_z) * cells_z + column % cells_z
    owner = column // cells_z % group
    index = jnp.arange(1, SIDE, dtype=jnp.int32)
    table = axis_table(index, where_z, length_z)
    part = jnp.arange(group, dtype=jnp.int32)
    inverse = jnp.where(part[:, None, None] == owner[None, None, :], table[None], 0.0)
    inverse = inverse.reshape(group * HALF, -1)
    forward = jnp.where(
        part[None, :, None] == owner[:, None, None], table.T[:, None, :], 0.0
    )
    forward = forward.reshape(-1, group * HALF)
    return split(inverse), jnp.concatenate(split(forward), axis=1)


def prepare_kernel(u_ref, v_ref, low_u_ref, low_v_ref, index_ref, out_ref, tall, low, tile):
    groups = u_ref.shape[0]
    levels = u_ref.shape[2]
    devices = out_ref.shape[0]
    rows = levels // devices
    step = rows * groups
    side = 2 * LANES
    eye = (
        lax.broadcasted_iota(jnp.int32, (side, side), 0)
        == lax.broadcasted_iota(jnp.int32, (side, side), 1)
    ).astype(bf16)
    for k, ref in enumerate((u_ref, v_ref)):
        for g in range(0, groups, 2):
            block = ref[g : g + 2].reshape(side, levels)
            for y in range(0, levels, side):
                turned = lax.dot_general(
                    eye,
                    block[:, y : y + side],
                    (((1,), (1,)), ((), ())),
                    preferred_element_type=f32,
                )
                tall[pl.ds(y * groups + g, side, stride=groups), :] = turned[:, :LANES]
                tall[pl.ds(y * groups + g + 1, side, stride=groups), :] = turned[:, LANES:]
        out_ref[:, k * step : (k + 1) * step, :] = (
            tall[...].astype(bf16).reshape(devices, step, LANES)
        )
    eye = eye[:LANES, :LANES]
    owned = low_u_ref.shape[0]
    for k, ref in enumerate((low_u_ref, low_v_ref)):
        padded = jnp.concatenate(
            [ref[...].astype(f32), jnp.zeros((LANES - owned, levels), f32)], axis=0
        ).astype(bf16)
        for y in range(0, levels, LANES):
            low[pl.ds(y, LANES), :] = lax.dot_general(
                eye,
                padded[:, y : y + LANES],
                (((1,), (1,)), ((), ())),
                preferred_element_type=f32,
            )
        for y in range(rows):
            tile[pl.ds(k * rows + y, devices, stride=groups), :] = (
                low[pl.ds(y, devices, stride=rows), :] + index_ref[...]
            )
    out_ref[:, 2 * step :, :] = tile[...].astype(bf16).reshape(devices, groups, LANES)


def middle_kernel(
    unitary,
    got_ref,
    back_x_ref,
    x_ref,
    top_ref,
    rest_ref,
    z_ref,
    out_ref,
    modes,
    left,
    right,
    spectrum,
    wave,
    mean,
    wave_top,
    wave_rest,
    products,
    sums,
    cross,
    coefficients,
    picked,
):
    groups_x, groups_z, _, _ = got_ref.shape
    groups = 8
    rows = 4
    owned = 16
    devices = groups_x * groups_z
    step = rows * groups
    points = groups_x * groups
    side = 2 * LANES
    lane = lax.broadcasted_iota(jnp.int32, (1, LANES), 1)
    low_half = lane < HALF

    modes[...] = got_ref[:, :, 2 * step :, :].astype(f32).reshape(devices * groups, LANES)
    first = modes[pl.ds(0, devices, stride=groups), :]
    turned = [first.T]
    for c in range(1, 2 * rows):
        turned.append(modes[pl.ds(c, devices, stride=groups), :].T)
    row = lax.broadcasted_iota(jnp.int32, (PADDED, devices), 0).astype(f32)
    column = lax.broadcasted_iota(jnp.int32, (devices, LANES), 1)
    wanted = (1 + column % HALF).astype(f32)
    for m in range(owned):
        at = slice(m * devices, (m + 1) * devices)
        hit = row == turned[0][owned + m : owned + m + 1, :]
        for c in range(2 * rows):
            left[c * PADDED : (c + 1) * PADDED, at] = jnp.where(
                hit, turned[c][m : m + 1, :], 0.0
            ).astype(bf16)
        left[2 * rows * PADDED :, at] = jnp.where(hit, 1.0, 0.0).astype(bf16)
        index_z = first[:, 2 * owned + m : 2 * owned + m + 1]
        right[at, :LANES] = jnp.where(wanted == index_z, 1.0, 0.0).astype(bf16)
        right[at, LANES:] = jnp.where(
            jnp.zeros((devices, LANES), f32) == index_z, 1.0, 0.0
        ).astype(bf16)
    spectrum[...] = dot(left[...], right[...]).astype(bf16)

    def spread(coefficient):
        full = dot(back_x_ref[...], jnp.concatenate([coefficient] * 2, axis=0))
        parts = [full[k * points : (k + 1) * points] for k in range(4)]
        waves = jnp.concatenate(
            [
                jnp.where(low_half, parts[0][:, :LANES], parts[1][:, :LANES]),
                jnp.where(low_half, parts[2][:, :LANES], parts[3][:, :LANES]),
            ],
            axis=1,
        )
        which = lane // (LANES // 4)
        constant = parts[3][:, LANES:]
        for k in range(3):
            constant = jnp.where(which == k, parts[k][:, LANES:], constant)
        return (
            waves.reshape(groups_x, groups, side),
            constant.reshape(groups_x, groups, LANES),
        )

    for c in range(2 * rows):
        waves, constant = spread(spectrum[c * PADDED : (c + 1) * PADDED, :])
        wave[c // rows, :, c % rows] = waves
        mean[c // rows, :, c % rows] = constant
    top, rest = halves(wave[...].reshape(2 * groups_x * step, side))
    wave_top[...] = top
    wave_rest[...] = rest
    sums[...] = jnp.zeros_like(sums)
    half_rows = groups_x * step

    def fine(j, k):
        parts = [
            got_ref[:, 2 * j + e, k * step : (k + 1) * step, :].reshape(half_rows, LANES)
            for e in range(2)
        ]
        return jnp.concatenate(parts, axis=1).astype(f32)

    def multiply(j, _):
        at = pl.ds(pl.multiple_of(j * side, side), side)
        coarse = (
            dot(wave_top[...], top_ref[:, at])
            + dot(wave_rest[...], top_ref[:, at])
            + dot(wave_top[...], rest_ref[:, at])
        )
        flat = mean[...].reshape(2 * half_rows, LANES)
        coarse = coarse + jnp.concatenate([flat, flat], axis=1)
        coarse_u, coarse_v = coarse[:half_rows], coarse[half_rows:]
        fine_u, fine_v = fine(j, 0), fine(j, 1)
        self_term = (coarse_u * coarse_v + fine_u * fine_v).astype(bf16)
        cross_term = coarse_u * fine_v + fine_u * coarse_v
        cross[:, at] = cross_term
        cross_round = cross_term.astype(bf16)
        products[:half_rows, at] = self_term
        products[half_rows:, at] = cross_round
        for k, term in enumerate((self_term, cross_round)):
            wide = term.astype(f32)
            sums[k] += (wide[:, :LANES] + wide[:, LANES:]).reshape(
                groups_x, rows, groups, LANES
            )
        return 0

    lax.fori_loop(0, groups_z // 2, multiply, 0)
    both = dot(products[...], z_ref[...])
    coefficients[...] = (both[:, :side] + both[:, side:]).reshape(
        2, groups_x, rows, groups, side
    )

    def project(k, y):
        waves = coefficients[k, :, y].reshape(points, side)
        total = sums[k, :, y].reshape(points, LANES)
        stack = []
        for part in range(4):
            half = waves[:, :LANES] if part < 2 else waves[:, LANES:]
            keep = low_half if part % 2 == 0 else jnp.logical_not(low_half)
            stack.append(
                jnp.concatenate(
                    [
                        jnp.where(keep, half, 0.0),
                        jnp.where(lane // (LANES // 4) == part, total, 0.0),
                    ],
                    axis=1,
                )
            )
        top, rest = halves(jnp.concatenate(stack, axis=0))
        outer = dot(x_ref[...], top)
        outer = outer[:PADDED] + outer[PADDED:] + dot(x_ref[:PADDED], rest)
        waves = outer[:, :LANES] * unitary
        waves = waves + pltpu.roll(waves, HALF, 1)
        constant = jnp.sum(outer[:, LANES:], axis=1, keepdims=True) * unitary
        return waves, jnp.broadcast_to(constant, (PADDED, LANES))

    row_index = lax.broadcasted_iota(jnp.int32, (PADDED, 1), 0)
    weight_x = jnp.where(row_index > 0, 2.0, 1.0).astype(f32)
    mask = spectrum[2 * rows * PADDED :, :]
    for y in range(rows):
        waves, constant = project(1, y)
        low = jnp.concatenate([waves * (2.0 * weight_x), constant * weight_x], axis=1)
        waves, constant = spread(low.astype(bf16) * mask)
        wave[0, :, y] = waves
        mean[0, :, y] = constant
    top, rest = halves(wave[0].reshape(half_rows, side))
    wave_top[:half_rows] = top
    wave_rest[:half_rows] = rest

    def subtract(j, _):
        at = pl.ds(pl.multiple_of(j * side, side), side)
        restored = dot(wave_top[:half_rows], top_ref[:, at]) + dot(
            wave_rest[:half_rows], top_ref[:, at]
        )
        flat = mean[0].reshape(half_rows, LANES)
        restored = restored + jnp.concatenate([flat, flat], axis=1)
        high = (cross[:, at] - unitary * restored).astype(bf16)
        for e in range(2):
            out_ref[:, 2 * j + e, :step, :] = high[:, e * LANES : (e + 1) * LANES].reshape(
                groups_x, step, LANES
            )
        return 0

    lax.fori_loop(0, groups_z // 2, subtract, 0)

    lines = 72
    parts = []
    for y in range(rows):
        waves, constant = project(0, y)
        force = jnp.where(low_half, waves, jnp.where(lane == HALF, constant, 0.0))
        force = jnp.concatenate([force, jnp.zeros((LANES - PADDED, LANES), f32)], axis=0)
        parts.append(force.T[:lines])
    force = jnp.concatenate(parts, axis=0).astype(bf16)[:, :PADDED]
    line = lax.broadcasted_iota(jnp.int32, (lines, devices), 0)
    line = jnp.where(line < HALF, line + 1, jnp.where(line == HALF, 0, -1)).astype(f32)
    picked[...] = jnp.zeros_like(picked)
    for m in range(0, owned, 2):
        chosen = dot(force, left[2 * rows * PADDED :, m * devices : (m + 2) * devices])
        for e in range(2):
            hit = line == turned[0][2 * owned + m + e : 2 * owned + m + e + 1, :]
            for y in range(rows):
                value = chosen[y * lines : (y + 1) * lines, e * devices : (e + 1) * devices]
                picked[y, m + e : m + e + 1, :] = jnp.sum(
                    jnp.where(hit, value, 0.0), axis=0, keepdims=True
                )
    modes[...] = jnp.zeros_like(modes)
    for y in range(rows):
        modes[pl.ds(y, devices, stride=groups), :] = picked[y].T
    out_ref[:, :, step:, :] = (
        modes[...].astype(bf16).reshape(groups_x, groups_z, groups, LANES)
    )


def on_device(high_u, high_v, low_u, low_v, low_kx, low_kz, tau_inverse):
    cells_x, cells_z, levels = high_u.shape
    owned = low_u.shape[0]
    groups_x = lax.axis_size("gx")
    groups_z = lax.axis_size("gz")
    devices = groups_x * groups_z
    length_x = groups_x * cells_x
    length_z = groups_z * cells_z
    rows = levels // devices
    group = LANES // cells_z
    groups = cells_x // group
    step = rows * groups
    points = groups_x * groups
    half_rows = groups_x * step
    width = groups_z * LANES
    side = 2 * LANES
    unitary = 1.0 / math.sqrt(length_x * length_z)

    index = jnp.concatenate(
        [jnp.zeros((owned,), f32), low_kx.astype(f32), low_kz.astype(f32)]
    )
    index = jnp.pad(index, (0, LANES - 3 * owned))[None, :]
    sent = pl.pallas_call(
        prepare_kernel,
        out_shape=jax.ShapeDtypeStruct((devices, 2 * step + groups, LANES), bf16),
        scratch_shapes=[
            pltpu.VMEM((levels * groups, LANES), f32),
            pltpu.VMEM((levels, LANES), f32),
            pltpu.VMEM((devices * groups, LANES), f32),
        ],
        compiler_params=pltpu.CompilerParams(vmem_limit_bytes=VMEM_LIMIT),
        interpret=INTERPRET,
        name="prepare",
    )(
        high_u.reshape(groups, LANES, levels),
        high_v.reshape(groups, LANES, levels),
        low_u,
        low_v,
        index,
    )
    got = lax.all_to_all(sent, AXES, 0, 0, tiled=True)

    forward_x, back_x = x_tables(groups_x, groups, group, length_x)
    (top, rest), forward_z = z_tables(group, cells_z, length_z)
    sent = pl.pallas_call(
        functools.partial(middle_kernel, unitary),
        out_shape=jax.ShapeDtypeStruct((groups_x, groups_z, step + groups, LANES), bf16),
        scratch_shapes=[
            pltpu.VMEM((devices * groups, LANES), f32),
            pltpu.VMEM(((2 * rows + 1) * PADDED, owned * devices), bf16),
            pltpu.VMEM((owned * devices, side), bf16),
            pltpu.VMEM(((2 * rows + 1) * PADDED, side), bf16),
            pltpu.VMEM((2, groups_x, rows, groups, side), f32),
            pltpu.VMEM((2, groups_x, rows, groups, LANES), f32),
            pltpu.VMEM((2 * half_rows, side), bf16),
            pltpu.VMEM((2 * half_rows, side), bf16),
            pltpu.VMEM((2 * half_rows, width), bf16),
            pltpu.VMEM((2, groups_x, rows, groups, LANES), f32),
            pltpu.VMEM((half_rows, width), f32),
            pltpu.VMEM((2, groups_x, rows, groups, side), f32),
            pltpu.VMEM((rows, LANES, devices), f32),
        ],
        compiler_params=pltpu.CompilerParams(vmem_limit_bytes=VMEM_LIMIT),
        interpret=INTERPRET,
        name="middle",
    )(
        got.reshape(groups_x, groups_z, 2 * step + groups, LANES),
        back_x,
        forward_x,
        top,
        rest,
        forward_z,
    )
    got = lax.all_to_all(
        sent.reshape(devices, step + groups, LANES), AXES, 0, 0, tiled=True
    )

    high_term = got[:, :step].reshape(levels, groups, LANES).transpose(1, 2, 0)
    high_term = high_term.reshape(cells_x, cells_z, levels)
    forcing = got[:, step : step + rows, :owned].reshape(levels, owned).T
    low_response = jnp.einsum(
        "mij,mj->mi", tau_inverse, forcing, preferred_element_type=f32
    )
    return (high_term, low_response)


def solution(mesh):
    placed = (
        P("gx", "gz", None),
        P("gx", "gz", None),
        P(AXES, None),
        P(AXES, None),
        P(AXES),
        P(AXES),
        P(AXES, None, None),
    )
    return jax.shard_map(
        on_device,
        mesh=mesh,
        in_specs=placed,
        out_specs=(P("gx", "gz", None), P(AXES, None)),
        check_vma=False,
    )
```

profile of v0, /device:TPU:1, one launch (start us, length us, event | category | flops | bytes accessed | tf_op | source)
XLA Modules:
  0.0 103.4 jit_solution(12278534185197483353)
XLA Ops:
  0.6 0.7 convert_element_type.61
  1.3 0.7 convert_element_type.60
  1.9 0.1 fusion.28.index_ref
  2.0 0.0 copy-start.1
  2.0 1.2 %copy-done.1 = bf16[32,32,512]{2,1,0:T(8,128)(2,1)S(1)} copy-done((bf16[32,32,512]{2,1,0:T(8,128)(2,1)S(1)}, bf16[32,32,512]{2,1,0:T(8,128)(2,1)}, u32[]{:S(2)}) %copy-start.1) | copy-done | bytes 1048600
  3.3 0.0 copy-start.2
  3.3 1.2 %copy-done.2 = bf16[32,32,512]{2,1,0:T(8,128)(2,1)S(1)} copy-done((bf16[32,32,512]{2,1,0:T(8,128)(2,1)S(1)}, bf16[32,32,512]{2,1,0:T(8,128)(2,1)}, u32[]{:S(2)}) %copy-start.2) | copy-done | bytes 1048600
  4.5 0.0 copy-start.3
  4.5 0.7 copy-done.3
  5.2 0.0 copy-start.4
  5.2 0.7 copy-done.4
  5.9 2.9 %prepare.1 = bf16[128,72,128]{2,1,0:T(8,128)(2,1)} custom-call(bf16[8,128,512]{2,1,0:T(8,128)(2,1)S(1)} %bitcast.25, bf16[8,128,512]{2,1,0:T(8,128)(2,1)S(1)} %bitcast.26, bf16[16,512]{1,0:T(8,128)(2,1)S(1)} %copy-done.3, bf16[16,512]{1,0:T(8,128)(2,1)S(1)} %copy-done.4, f32[1,128]{1,0:T(1,128)S(1)} %fusion.28.index_ref), custom_call_target="tpu_custom_call" | custom-call | tf_op jit(solution)/shard_map/prepare/pallas_call | solution.py:346
  8.8 11.9 %all-to-all-start = ((bf16[128,72,128]{2,1,0:T(8,128)(2,1)}), bf16[128,72,128]{2,1,0:T(8,128)(2,1)}, u32[]{:S(2)}, u32[]{:S(2)}) async-start(bf16[128,72,128]{2,1,0:T(8,128)(2,1)} %prepare.1), calls=%async_computation | async-start | bytes 4718592 | tf_op jit(solution)/shard_map/all_to_all | solution.py:364
  20.7 0.1 broadcast_add_fusion
  20.8 0.1 add.214
  20.9 0.6 reduce-precision_convert_fusion.2
  21.5 0.4 reduce-precision_convert_fusion.3
  22.0 2.1 %sine_select_fusion = f32[2048,64]{0,1:T(8,128)S(1)} fusion(s32[2048]{0:T(1024)S(1)} %fusion.25, s32[64]{0:T(128)S(1)} %add_select_fusion.8, pred[64]{0:T(512)(128)(4,1)S(1)} %fusion.29), kind=kLoop, calls=%fused_computation.25 | loop fusion | flops 1966080 | bytes 532800 | tf_op jit(solution)/shard_map/jit(_where)/select_n | solution.py:27
  24.2 0.2 broadcast_select_fusion
  24.4 1.9 %copy.10 = f32[2048,256]{1,0:T(8,128)} copy(f32[2048,256]{0,1:T(8,128)S(1)} %bitcast.27) | data formatting | bytes 4194304 | tf_op jit(solution)/shard_map/jit(_where)/select_n | solution.py:67
  26.3 1.9 %reduce-precision_convert_fusion = (bf16[2048,256]{1,0:T(8,128)(2,1)S(1)}, bf16[2048,256]{1,0:T(8,128)(2,1)S(1)}) fusion(f32[2048,256]{1,0:T(8,128)} %copy.10), kind=kLoop, calls=%fused_computation.1 | loop fusion | flops 2097152 | bytes 4194304 | tf_op jit(solution)/shard_map/convert_element_type | solution.py:32
  28.2 0.1 pad_maximum_fusion.1.back_x_ref
  28.3 0.2 pad_maximum_fusion.z_ref
  28.5 2.1 %sine_select_fusion.1 = f32[64,2048]{1,0:T(8,128)S(1)} fusion(s32[2048]{0:T(1024)S(1)} %fusion.25, s32[64]{0:T(128)S(1)} %add_select_fusion.8, pred[64]{0:T(512)(128)(4,1)S(1)} %fusion.29), kind=kLoop, calls=%fused_computation.26 | loop fusion | flops 1966080 | bytes 532800 | tf_op jit(solution)/shard_map/jit(_where)/select_n | solution.py:27
  30.7 0.3 broadcast_select_fusion.1
  30.9 1.3 %fusion = (bf16[256,2048]{1,0:T(8,128)(2,1)S(1)}, bf16[256,2048]{1,0:T(8,128)(2,1)}) fusion(f32[4,64,2048]{2,1,0:T(8,128)S(1)} %broadcast_select_fusion.1), kind=kLoop, calls=%fused_computation.4 | loop fusion | flops 2097152 | bytes 4194304 | tf_op jit(solution)/shard_map/convert_element_type | solution.py:32
  32.2 21.6 %all-to-all-done = bf16[128,72,128]{2,1,0:T(8,128)(2,1)} async-done(((bf16[128,72,128]{2,1,0:T(8,128)(2,1)}), bf16[128,72,128]{2,1,0:T(8,128)(2,1)}, u32[]{:S(2)}, u32[]{:S(2)}) %all-to-all-start) | async-done | bytes 2359328 | tf_op jit(solution)/shard_map/all_to_all | solution.py:364
  53.8 0.0 copy-start
  53.8 1.2 %copy-done = bf16[256,2048]{1,0:T(8,128)(2,1)S(1)} copy-done((bf16[256,2048]{1,0:T(8,128)(2,1)S(1)}, bf16[256,2048]{1,0:T(8,128)(2,1)}, u32[]{:S(2)}) %copy-start) | copy-done | bytes 1048600
  55.1 14.1 %middle.1 = bf16[8,16,40,128]{3,2,1,0:T(8,128)(2,1)S(1)} custom-call(bf16[8,16,72,128]{3,2,1,0:T(8,128)(2,1)} %bitcast.3.got_ref, bf16[256,160]{1,0:T(8,128)(2,1)S(1)} %pad_maximum_fusion.1.back_x_ref, bf16[160,256]{1,0:T(8,128)(2,1)S(1)} %pad_maximum_fusion.2.x_ref, bf16[256,2048]{1,0:T(8,128)(2,1)S(1)} %copy-done, ...), custom_call_target="tpu_custom_call" | custom-call | tf_op jit(solution)/shard_map/middle/pallas_call | solution.py:368
  69.2 26.2 %all_to_all.10 = bf16[128,40,128]{2,1,0:T(8,128)(2,1)S(1)} all-to-all(bf16[128,40,128]{2,1,0:T(8,128)(2,1)S(1)} %bitcast.24), channel_id=1, replica_groups=mesh['gx'=8,'gz'=16] {'gx','gz'}, dimensions={0} | all-to-all | bytes 2621440 | tf_op jit(solution)/shard_map/all_to_all | solution.py:397
  95.4 0.1 slice.8
  95.5 1.5 %copy.12 = bf16[512,8,128]{0,2,1:T(8,128)(2,1)} copy(bf16[512,8,128]{2,1,0:T(8,128)(2,1)S(1)} %bitcast.28) | data formatting | bytes 2097152 | tf_op jit(solution)/shard_map/reshape | solution.py:401
  97.0 0.1 copy.13
  97.2 5.6 %fusion.30 = f32[16,1,512]{2,1,0:T(1,128)S(1)} fusion(bf16[16,512,1]{1,2,0:T(2,128)(2,1)S(1)} %copy.13, bf16[16,512,512]{2,1,0:T(8,128)(2,1)} %param.13), kind=kOutput, calls=%fused_computation.92 | convolution fusion | flops 8388608 | bytes 8437760 | tf_op jit(solution)/shard_map/mij,mj->mi/dot_general | solution.py:404
  102.8 0.6 copy.16
  (13 shorter events, 0.1 us)
Async XLA Ops:
  2.0 1.2 %copy-start.1 = (bf16[32,32,512]{2,1,0:T(8,128)(2,1)S(1)}, bf16[32,32,512]{2,1,0:T(8,128)(2,1)}, u32[]{:S(2)}) copy-start(bf16[32,32,512]{2,1,0:T(8,128)(2,1)} %param.7) | copy-start | bytes 3145732
  3.3 1.2 %copy-start.2 = (bf16[32,32,512]{2,1,0:T(8,128)(2,1)S(1)}, bf16[32,32,512]{2,1,0:T(8,128)(2,1)}, u32[]{:S(2)}) copy-start(bf16[32,32,512]{2,1,0:T(8,128)(2,1)} %param.8) | copy-start | bytes 3145732
  4.5 0.7 copy-start.3
  5.2 0.7 copy-start.4
  8.8 45.1 %all-to-all-start = ((bf16[128,72,128]{2,1,0:T(8,128)(2,1)}), bf16[128,72,128]{2,1,0:T(8,128)(2,1)}, u32[]{:S(2)}, u32[]{:S(2)}) async-start(bf16[128,72,128]{2,1,0:T(8,128)(2,1)} %prepare.1), calls=%async_computation | async-start | bytes 4718592 | tf_op jit(solution)/shard_map/all_to_all | solution.py:364
  53.8 1.2 %copy-start = (bf16[256,2048]{1,0:T(8,128)(2,1)S(1)}, bf16[256,2048]{1,0:T(8,128)(2,1)}, u32[]{:S(2)}) copy-start(bf16[256,2048]{1,0:T(8,128)(2,1)} %get-tuple-element.5.top_ref) | copy-start | bytes 3145732
where the time goes:
time: 104 us; the launch traced here: 103 us
  blocking collectives  26.2 us (25%)
  waiting for transfers between devices  21.6 us (21%)
  Pallas kernels  17 us (16%)
  starting transfers between devices  11.9 us (11%)
  other arithmetic  10.8 us (10%)
  local copies, waits for them, and re-layouts  9.41 us (9%)
  matrix products  5.64 us (5%)
    all_to_all x1, blocking collectives, on_device(): lax.all_to_all(sent.reshape(devices, step + groups, LANES), AXES, 0, 0, t...  26.2 us
    all_to_all x1, waiting for transfers between devices, on_device(): got = lax.all_to_all(sent, AXES, 0, 0, tiled=True)  21.6 us
    pallas_call x1, Pallas kernels, on_device(): pl.pallas_call(functools.partial(middle_kernel, unitary), out_shape=jax.S...  14.1 us
    all_to_all x1, starting transfers between devices, on_device(): got = lax.all_to_all(sent, AXES, 0, 0, tiled=True)  11.9 us
    dot_general x1, matrix products, on_device(): jnp.einsum('mij,mj->mi', tau_inverse, forcing, preferred_element_type=f32)  5.64 us
    unnamed x10, local copies, waits for them, and re-layouts  5.11 us
    select_n x2, other arithmetic, axis_table(): return jnp.where((index <= KL)[:, None], jnp.cos(angles), jnp.sin(angles))  4.28 us
    convert_element_type x4, other arithmetic, split(): return (top.astype(bf16), (values - top).astype(bf16))  4.25 us
  transfers between devices with their start and end apart: 1, of which 1 were waited for; matrix products, arithmetic and copies ran while one was open for 11% of the time, Pallas kernels for 0%

commit v1 on v0

v1 whole, which is shorter than its diff:
```python
import functools
import math

import jax
import jax.numpy as jnp
from jax import lax
from jax.experimental import pallas as pl
from jax.experimental.pallas import tpu as pltpu
from jax.sharding import PartitionSpec as P

KL = 32
SIDE = 2 * KL + 1
PADDED = 80
LANES = 128
HALF = LANES // 2
AXES = ("gx", "gz")
INTERPRET = False
WHOLE = 67043328
UNROLL = 1
bf16 = jnp.bfloat16
f32 = jnp.float32


def axis_table(index, positions, length):
    wavenum = jnp.where(index <= KL, index, index - KL)
    phases = wavenum[:, None] * positions[None, :] % length
    angles = phases.astype(f32) * (2.0 * math.pi / length)
    return jnp.where((index <= KL)[:, None], jnp.cos(angles), jnp.sin(angles))


def split(values):
    top = lax.reduce_precision(values, 8, 7)
    return top.astype(bf16), (values - top).astype(bf16)


def halves(values):
    top = values.astype(bf16)
    return top, (values - top.astype(f32)).astype(bf16)


def dot(a, b):
    return jnp.dot(a, b, preferred_element_type=f32)


def x_tables(groups_x, groups, group, length_x):
    part = jnp.arange(group, dtype=jnp.int32)[:, None, None]
    device = jnp.arange(groups_x, dtype=jnp.int32)[None, :, None]
    block = jnp.arange(groups, dtype=jnp.int32)[None, None, :]
    where_x = (device * (group * groups) + block * group + part).reshape(-1)
    index = jnp.arange(PADDED, dtype=jnp.int32)
    table = axis_table(index, where_x, length_x)
    table = jnp.where((index < SIDE)[:, None], table, 0.0)
    top, rest = split(table)
    forward = jnp.concatenate([top, rest], axis=0)
    top, rest = split(table.T)
    return forward, jnp.concatenate([top, rest], axis=1)


def z_tables(group, cells_z, length_z):
    column = jnp.arange(length_z * group, dtype=jnp.int32)
    where_z = column // (group * cells_z) * cells_z + column % cells_z
    owner = column // cells_z % group
    index = jnp.arange(1, SIDE, dtype=jnp.int32)
    table = axis_table(index, where_z, length_z)
    part = jnp.arange(group, dtype=jnp.int32)
    inverse = jnp.where(part[:, None, None] == owner[None, None, :], table[None], 0.0)
    inverse = inverse.reshape(group * HALF, -1)
    forward = jnp.where(
        part[None, :, None] == owner[:, None, None], table.T[:, None, :], 0.0
    )
    forward = forward.reshape(-1, group * HALF)
    return inverse.astype(bf16), split(forward)


def across(eye, block):
    return lax.dot_general(
        eye, block, (((1,), (1,)), ((), ())), preferred_element_type=f32
    )


def identity(size):
    return (
        lax.broadcasted_iota(jnp.int32, (size, size), 0)
        == lax.broadcasted_iota(jnp.int32, (size, size), 1)
    ).astype(bf16)


def prepare_kernel(
    u_ref,
    v_ref,
    low_u_ref,
    low_v_ref,
    kx_ref,
    kz_ref,
    out_ref,
    fine,
    lows,
    index,
    tall,
    low,
    tile,
    ready,
    fine_sem,
    low_sem,
    index_sem,
    out_sem,
):
    groups, _, levels = u_ref.shape
    owned = low_u_ref.shape[0]
    devices = out_ref.shape[0]
    rows = levels // devices
    step = rows * groups
    side = 2 * LANES
    pairs = groups // 2
    copies = []
    for k, ref in enumerate((kx_ref, kz_ref)):
        copies.append(pltpu.make_async_copy(ref, index.at[k], index_sem.at[k]))
    for k, ref in enumerate((low_u_ref, low_v_ref)):
        copies.append(pltpu.make_async_copy(ref, lows.at[k], low_sem.at[k]))
    for k, ref in enumerate((u_ref, v_ref)):
        for g in range(pairs):
            at = pl.ds(2 * g, 2)
            copies.append(
                pltpu.make_async_copy(ref.at[at], fine.at[k, at], fine_sem.at[k, g])
            )
    for copy in copies:
        copy.start()
    for copy in copies[:4]:
        copy.wait()

    def send(k, first, count):
        part = (slice(None), pl.ds(first, count))
        return pltpu.make_async_copy(ready.at[part], out_ref.at[part], out_sem.at[k])

    lane = lax.broadcasted_iota(jnp.int32, (1, LANES), 1)
    line = jnp.zeros((1, LANES), f32)
    for m in range(owned):
        line = jnp.where(lane == owned + m, index[0, m].astype(f32), line)
        line = jnp.where(lane == 2 * owned + m, index[1, m].astype(f32), line)
    eye = identity(LANES)
    for k in range(2):
        padded = jnp.concatenate(
            [lows[k].astype(f32), jnp.zeros((LANES - owned, levels), f32)], axis=0
        ).astype(bf16)
        for y in range(0, levels, LANES):
            low[pl.ds(y, LANES), :] = across(eye, padded[:, y : y + LANES])
        for y in range(rows):
            tile[pl.ds(k * rows + y, devices, stride=groups), :] = (
                low[pl.ds(y, devices, stride=rows), :] + line
            )
    ready[:, 2 * step :, :] = tile[...].astype(bf16).reshape(devices, groups, LANES)
    sends = [send(2, 2 * step, groups)]
    sends[0].start()
    eye = identity(side)
    for k in range(2):
        for g in range(pairs):
            copies[4 + k * pairs + g].wait()
            block = fine[k, 2 * g : 2 * g + 2].reshape(side, levels)
            for y in range(0, levels, side):
                turned = across(eye, block[:, y : y + side])
                at = y * groups + 2 * g
                tall[pl.ds(at, side, stride=groups), :] = turned[:, :LANES]
                tall[pl.ds(at + 1, side, stride=groups), :] = turned[:, LANES:]
        ready[:, k * step : (k + 1) * step, :] = (
            tall[...].astype(bf16).reshape(devices, step, LANES)
        )
        sends.append(send(k, k * step, step))
        sends[-1].start()
    for copy in sends:
        copy.wait()


def middle_kernel(
    unitary,
    got_hbm,
    back_x_hbm,
    x_hbm,
    top_hbm,
    z_top_hbm,
    z_rest_hbm,
    out_hbm,
    got_ref,
    back_x_ref,
    x_ref,
    top_ref,
    z_top_ref,
    z_rest_ref,
    out_ref,
    modes,
    left,
    right,
    spectrum,
    wave,
    mean,
    wave_top,
    products,
    sums,
    cross,
    coefficients,
    picked,
    in_sem,
    out_sem,
):
    groups_x, groups_z, _, _ = got_ref.shape
    groups = 8
    rows = 4
    owned = 16
    devices = groups_x * groups_z
    step = rows * groups
    points = groups_x * groups
    side = 2 * LANES
    half_rows = groups_x * step
    lane = lax.broadcasted_iota(jnp.int32, (1, LANES), 1)
    low_half = lane < HALF
    which = lane // (LANES // 4)

    everything = (slice(None), slice(None))
    tiles = everything + (pl.ds(2 * step, groups),)
    lines = everything + (pl.ds(0, 2 * step),)
    fetches = [
        pltpu.make_async_copy(source, target, in_sem.at[k])
        for k, (source, target) in enumerate(
            (
                (got_hbm.at[tiles], got_ref.at[tiles]),
                (back_x_hbm, back_x_ref),
                (top_hbm, top_ref),
                (got_hbm.at[lines], got_ref.at[lines]),
                (x_hbm, x_ref),
                (z_top_hbm, z_top_ref),
                (z_rest_hbm, z_rest_ref),
            )
        )
    ]
    for fetch in fetches:
        fetch.start()
    fetches[0].wait()
    modes[...] = got_ref[:, :, 2 * step :, :].astype(f32).reshape(devices * groups, LANES)
    first = modes[pl.ds(0, devices, stride=groups), :]
    turned = [first.T]
    for c in range(1, 2 * rows):
        turned.append(modes[pl.ds(c, devices, stride=groups), :].T)
    row = lax.broadcasted_iota(jnp.int32, (PADDED, devices), 0).astype(f32)
    column = lax.broadcasted_iota(jnp.int32, (devices, LANES), 1)
    wanted = (1 + column % HALF).astype(f32)
    for m in range(owned):
        at = slice(m * devices, (m + 1) * devices)
        hit = row == turned[0][owned + m : owned + m + 1, :]
        hit = jnp.where(hit, 1.0, 0.0).astype(bf16)
        for c in range(2 * rows):
            value = jnp.broadcast_to(turned[c][m : m + 1, :], (16, devices)).astype(bf16)
            value = jnp.concatenate([value] * (PADDED // 16), axis=0)
            left[c * PADDED : (c + 1) * PADDED, at] = hit * value
        left[2 * rows * PADDED :, at] = hit
        index_z = jnp.broadcast_to(
            first[:, 2 * owned + m : 2 * owned + m + 1], (devices, LANES)
        )
        right[at, :LANES] = jnp.where(wanted == index_z, 1.0, 0.0).astype(bf16)
        right[at, LANES:] = jnp.where(index_z == 0.0, 1.0, 0.0).astype(bf16)
    spectrum[...] = dot(left[...], right[...]).astype(bf16)
    fetches[1].wait()

    def spread(k, parts):
        both = jnp.concatenate(parts, axis=1)
        full = dot(back_x_ref[...], jnp.concatenate([both, both], axis=0))
        for y in range(len(parts)):
            part = [
                full[p * points : (p + 1) * points, y * side : (y + 1) * side]
                for p in range(4)
            ]
            waves = jnp.concatenate(
                [
                    jnp.where(low_half, part[0][:, :LANES], part[1][:, :LANES]),
                    jnp.where(low_half, part[2][:, :LANES], part[3][:, :LANES]),
                ],
                axis=1,
            )
            constant = part[3][:, LANES:]
            for p in range(3):
                constant = jnp.where(which == p, part[p][:, LANES:], constant)
            wave[k, :, y] = waves.reshape(groups_x, groups, side)
            mean[k, :, y] = constant.reshape(groups_x, groups, LANES)

    for k in range(2):
        spread(
            k,
            [
                spectrum[(k * rows + y) * PADDED : (k * rows + y + 1) * PADDED, :]
                for y in range(rows)
            ],
        )
    wave_top[...] = wave[...].reshape(2 * half_rows, side).astype(bf16)
    sums[...] = jnp.zeros_like(sums)
    fetches[2].wait()
    fetches[3].wait()

    def fine(j, k):
        parts = [
            got_ref[:, 2 * j + e, k * step : (k + 1) * step, :].reshape(half_rows, LANES)
            for e in range(2)
        ]
        return jnp.concatenate(parts, axis=1).astype(f32)

    def multiply(j, _):
        at = pl.ds(pl.multiple_of(j * side, side), side)
        coarse = dot(wave_top[...], top_ref[:, at])
        flat = mean[...].reshape(2 * half_rows, LANES)
        coarse = coarse + jnp.concatenate([flat, flat], axis=1)
        coarse_u, coarse_v = coarse[:half_rows], coarse[half_rows:]
        fine_u, fine_v = fine(j, 0), fine(j, 1)
        self_term = (coarse_u * coarse_v + fine_u * fine_v).astype(bf16)
        cross_term = coarse_u * fine_v + fine_u * coarse_v
        cross[:, at] = cross_term
        cross_round = cross_term.astype(bf16)
        products[:half_rows, at] = self_term
        products[half_rows:, at] = cross_round
        for k, term in enumerate((self_term, cross_round)):
            wide = term.astype(f32)
            sums[k] += (wide[:, :LANES] + wide[:, LANES:]).reshape(
                groups_x, rows, groups, LANES
            )
        return 0

    lax.fori_loop(0, groups_z // 2, multiply, 0, unroll=UNROLL)
    for fetch in fetches[4:]:
        fetch.wait()
    both = dot(products[...], z_top_ref[...]) + dot(products[...], z_rest_ref[...])
    coefficients[...] = both.reshape(2, groups_x, rows, groups, side)

    def project(k):
        stacks = []
        for y in range(rows):
            waves = coefficients[k, :, y].reshape(points, side)
            total = sums[k, :, y].reshape(points, LANES)
            stack = []
            for part in range(4):
                half = waves[:, :LANES] if part < 2 else waves[:, LANES:]
                keep = low_half if part % 2 == 0 else jnp.logical_not(low_half)
                stack.append(
                    jnp.concatenate(
                        [
                            jnp.where(keep, half, 0.0),
                            jnp.where(which == part, total, 0.0),
                        ],
                        axis=1,
                    )
                )
            stacks.append(jnp.concatenate(stack, axis=0))
        top, rest = halves(jnp.concatenate(stacks, axis=1))
        outer = dot(x_ref[...], top)
        outer = outer[:PADDED] + outer[PADDED:] + dot(x_ref[:PADDED], rest)
        done = []
        for y in range(rows):
            waves = outer[:, y * side : y * side + LANES] * unitary
            waves = waves + pltpu.roll(waves, HALF, 1)
            constant = outer[:, y * side + LANES : (y + 1) * side]
            constant = jnp.sum(constant, axis=1, keepdims=True) * unitary
            done.append((waves, jnp.broadcast_to(constant, (PADDED, LANES))))
        return done

    row_index = lax.broadcasted_iota(jnp.int32, (PADDED, 1), 0)
    weight_x = jnp.where(row_index > 0, 2.0, 1.0).astype(f32)
    mask = spectrum[2 * rows * PADDED :, :]
    parts = []
    for waves, constant in project(1):
        low = jnp.concatenate([waves * (2.0 * weight_x), constant * weight_x], axis=1)
        parts.append(low.astype(bf16) * mask)
    spread(0, parts)
    wave_top[:half_rows] = wave[0].reshape(half_rows, side).astype(bf16)

    kept = 72
    parts = []
    for waves, constant in project(0):
        force = jnp.where(low_half, waves, jnp.where(lane == HALF, constant, 0.0))
        force = jnp.concatenate([force, jnp.zeros((LANES - PADDED, LANES), f32)], axis=0)
        parts.append(force.T[:kept])
    force = jnp.concatenate(parts, axis=0).astype(bf16)[:, :PADDED]
    line = lax.broadcasted_iota(jnp.int32, (kept, devices), 0)
    line = jnp.where(line < HALF, line + 1, jnp.where(line == HALF, 0, -1)).astype(f32)
    picked[...] = jnp.zeros_like(picked)
    for m in range(0, owned, 2):
        chosen = dot(force, left[2 * rows * PADDED :, m * devices : (m + 2) * devices])
        for e in range(2):
            hit = line == turned[0][2 * owned + m + e : 2 * owned + m + e + 1, :]
            for y in range(rows):
                value = chosen[y * kept : (y + 1) * kept, e * devices : (e + 1) * devices]
                picked[y, m + e : m + e + 1, :] = jnp.sum(
                    jnp.where(hit, value, 0.0), axis=0, keepdims=True
                )
    modes[...] = jnp.zeros_like(modes)
    for y in range(rows):
        modes[pl.ds(y, devices, stride=groups), :] = picked[y].T
    out_ref[:, :, step:, :] = (
        modes[...].astype(bf16).reshape(groups_x, groups_z, groups, LANES)
    )
    part = everything + (pl.ds(step, groups),)
    send_tiles = pltpu.make_async_copy(
        out_ref.at[part], out_hbm.at[part], out_sem.at[groups_z // 2]
    )
    send_tiles.start()

    def send(j):
        part = (slice(None), pl.ds(2 * j, 2), pl.ds(0, step))
        return pltpu.make_async_copy(out_ref.at[part], out_hbm.at[part], out_sem.at[j])

    def subtract(j, _):
        at = pl.ds(pl.multiple_of(j * side, side), side)
        restored = dot(wave_top[:half_rows], top_ref[:, at])
        flat = mean[0].reshape(half_rows, LANES)
        restored = restored + jnp.concatenate([flat, flat], axis=1)
        high = (cross[:, at] - unitary * restored).astype(bf16)
        for e in range(2):
            out_ref[:, 2 * j + e, :step, :] = high[:, e * LANES : (e + 1) * LANES].reshape(
                groups_x, step, LANES
            )
        send(j).start()
        return 0

    lax.fori_loop(0, groups_z // 2, subtract, 0, unroll=UNROLL)
    send_tiles.wait()

    def drain(j, _):
        send(j).wait()
        return 0

    lax.fori_loop(0, groups_z // 2, drain, 0)


def finish_kernel(
    got_hbm,
    tau_hbm,
    high_hbm,
    low_ref,
    got_ref,
    tau_ref,
    tall,
    tile,
    force,
    ready,
    got_sem,
    tau_sem,
    out_sem,
):
    devices = got_hbm.shape[0]
    owned, levels, _ = tau_hbm.shape
    rows = levels // devices
    groups = high_hbm.shape[0]
    step = rows * groups
    chunk = LANES // rows
    count = devices // chunk
    fetches = []
    for q in range(count):
        at = pl.ds(q * chunk, chunk)
        fetches.append(
            pltpu.make_async_copy(got_hbm.at[at], got_ref.at[at], got_sem.at[q])
        )
    for m in range(owned):
        fetches.append(
            pltpu.make_async_copy(tau_hbm.at[m], tau_ref.at[m], tau_sem.at[m])
        )
    for fetch in fetches:
        fetch.start()
    eye = identity(LANES)
    sends = []
    for q in range(count):
        fetches[q].wait()
        at = slice(q * chunk, (q + 1) * chunk)
        tall[...] = got_ref[at, :step, :].astype(f32).reshape(chunk * step, LANES)
        where = pl.ds(q * LANES, LANES)
        for g in range(groups):
            column = tall[pl.ds(g, LANES, stride=groups), :].astype(bf16)
            ready[g, :, q * LANES : (q + 1) * LANES] = across(eye, column).astype(bf16)
        part = (slice(None), slice(None), where)
        sends.append(
            pltpu.make_async_copy(ready.at[part], high_hbm.at[part], out_sem.at[q])
        )
        sends[-1].start()
    tile[...] = got_ref[:, step:, :].astype(f32).reshape(devices * groups, LANES)
    for y in range(rows):
        force[pl.ds(y, devices, stride=rows), :] = tile[
            pl.ds(y, devices, stride=groups), :
        ]
    vector = force[...].astype(bf16)
    lane = lax.broadcasted_iota(jnp.int32, (levels, LANES), 1)
    answer = jnp.zeros((levels, LANES), f32)
    for m in range(owned):
        fetches[count + m].wait()
        answer = jnp.where(lane == m, dot(tau_ref[m], vector), answer)
    low_ref[...] = answer.T[:owned]
    for copy in sends:
        copy.wait()


def on_device(high_u, high_v, low_u, low_v, low_kx, low_kz, tau_inverse):
    cells_x, cells_z, levels = high_u.shape
    owned = low_u.shape[0]
    groups_x = lax.axis_size("gx")
    groups_z = lax.axis_size("gz")
    devices = groups_x * groups_z
    length_x = groups_x * cells_x
    length_z = groups_z * cells_z
    rows = levels // devices
    group = LANES // cells_z
    groups = cells_x // group
    step = rows * groups
    points = groups_x * groups
    half_rows = groups_x * step
    width = groups_z * LANES
    side = 2 * LANES
    unitary = 1.0 / math.sqrt(length_x * length_z)

    anywhere = pl.BlockSpec(memory_space=pltpu.HBM)
    sent = pl.pallas_call(
        prepare_kernel,
        out_shape=jax.ShapeDtypeStruct((devices, 2 * step + groups, LANES), bf16),
        in_specs=[anywhere] * 6,
        out_specs=anywhere,
        scratch_shapes=[
            pltpu.VMEM((2, groups, LANES, levels), bf16),
            pltpu.VMEM((2, owned, levels), bf16),
            pltpu.SMEM((2, owned), jnp.int32),
            pltpu.VMEM((levels * groups, LANES), f32),
            pltpu.VMEM((levels, LANES), f32),
            pltpu.VMEM((devices * groups, LANES), f32),
            pltpu.VMEM((devices, 2 * step + groups, LANES), bf16),
            pltpu.SemaphoreType.DMA((2, groups // 2)),
            pltpu.SemaphoreType.DMA((2,)),
            pltpu.SemaphoreType.DMA((2,)),
            pltpu.SemaphoreType.DMA((3,)),
        ],
        compiler_params=pltpu.CompilerParams(vmem_limit_bytes=WHOLE),
        interpret=INTERPRET,
        name="prepare",
    )(
        high_u.reshape(groups, LANES, levels),
        high_v.reshape(groups, LANES, levels),
        low_u,
        low_v,
        low_kx,
        low_kz,
    )
    got = lax.all_to_all(sent, AXES, 0, 0, tiled=True)

    forward_x, back_x = x_tables(groups_x, groups, group, length_x)
    top, forward_z = z_tables(group, cells_z, length_z)
    sent = pl.pallas_call(
        functools.partial(middle_kernel, unitary),
        out_shape=jax.ShapeDtypeStruct((groups_x, groups_z, step + groups, LANES), bf16),
        in_specs=[anywhere] * 6,
        out_specs=anywhere,
        scratch_shapes=[
            pltpu.VMEM((groups_x, groups_z, 2 * step + groups, LANES), bf16),
            pltpu.VMEM(back_x.shape, bf16),
            pltpu.VMEM(forward_x.shape, bf16),
            pltpu.VMEM(top.shape, bf16),
            pltpu.VMEM(forward_z[0].shape, bf16),
            pltpu.VMEM(forward_z[1].shape, bf16),
            pltpu.VMEM((groups_x, groups_z, step + groups, LANES), bf16),
            pltpu.VMEM((devices * groups, LANES), f32),
            pltpu.VMEM(((2 * rows + 1) * PADDED, owned * devices), bf16),
            pltpu.VMEM((owned * devices, side), bf16),
            pltpu.VMEM(((2 * rows + 1) * PADDED, side), bf16),
            pltpu.VMEM((2, groups_x, rows, groups, side), f32),
            pltpu.VMEM((2, groups_x, rows, groups, LANES), f32),
            pltpu.VMEM((2 * half_rows, side), bf16),
            pltpu.VMEM((2 * half_rows, width), bf16),
            pltpu.VMEM((2, groups_x, rows, groups, LANES), f32),
            pltpu.VMEM((half_rows, width), f32),
            pltpu.VMEM((2, groups_x, rows, groups, side), f32),
            pltpu.VMEM((rows, LANES, devices), f32),
            pltpu.SemaphoreType.DMA((7,)),
            pltpu.SemaphoreType.DMA((groups_z // 2 + 1,)),
        ],
        compiler_params=pltpu.CompilerParams(vmem_limit_bytes=WHOLE),
        interpret=INTERPRET,
        name="middle",
    )(
        got.reshape(groups_x, groups_z, 2 * step + groups, LANES),
        back_x,
        forward_x,
        top,
        *forward_z,
    )
    got = lax.all_to_all(
        sent.reshape(devices, step + groups, LANES), AXES, 0, 0, tiled=True
    )

    high_term, low_response = pl.pallas_call(
        finish_kernel,
        out_shape=(
            jax.ShapeDtypeStruct((groups, LANES, levels), bf16),
            jax.ShapeDtypeStruct((owned, levels), f32),
        ),
        in_specs=[anywhere] * 2,
        out_specs=(anywhere, pl.BlockSpec(memory_space=pltpu.VMEM)),
        scratch_shapes=[
            pltpu.VMEM((devices, step + groups, LANES), bf16),
            pltpu.VMEM((owned, levels, levels), bf16),
            pltpu.VMEM((LANES * groups, LANES), f32),
            pltpu.VMEM((devices * groups, LANES), f32),
            pltpu.VMEM((levels, LANES), f32),
            pltpu.VMEM((groups, LANES, levels), bf16),
            pltpu.SemaphoreType.DMA((devices * rows // LANES,)),
            pltpu.SemaphoreType.DMA((owned,)),
            pltpu.SemaphoreType.DMA((devices * rows // LANES,)),
        ],
        compiler_params=pltpu.CompilerParams(vmem_limit_bytes=WHOLE),
        interpret=INTERPRET,
        name="finish",
    )(got, tau_inverse)
    return (high_term.reshape(cells_x, cells_z, levels), low_response)


def solution(mesh):
    placed = (
        P("gx", "gz", None),
        P("gx", "gz", None),
        P(AXES, None),
        P(AXES, None),
        P(AXES),
        P(AXES),
        P(AXES, None, None),
    )
    return jax.shard_map(
        on_device,
        mesh=mesh,
        in_specs=placed,
        out_specs=(P("gx", "gz", None), P(AXES, None)),
        check_vma=False,
    )
```

time: 104 us -> 104 us (level)
  Pallas kernels: 17 us -> 29.8 us
  local copies, waits for them, and re-layouts: 9.41 us -> 1.97 us
  matrix products: 5.64 us -> 0 us
  blocking collectives: 26.2 us -> 27.8 us
    pallas_call x0 -> x1, Pallas kernels: none -> 11.8 us  [on_device(): pl.pallas_call(finish_kernel, out_shape=(jax.ShapeDtypeStruct((groups, LA...]
    dot_general x1 -> x0, matrix products: 5.64 us -> none  [on_device(): jnp.einsum('mij,mj->mi', tau_inverse, forcing, preferred_element_type=f32)]
    unnamed x10 -> x2, local copies, waits for them, and re-layouts: 5.11 us -> 0.01 us
    pallas_call x1, Pallas kernels: 2.88 us -> 5.28 us  [on_device(): pl.pallas_call(prepare_kernel, out_shape=jax.ShapeDtypeStruct((devices, 2...]
    all_to_all x1, blocking collectives: 26.2 us -> 27.8 us  [on_device(): lax.all_to_all(sent.reshape(devices, step + groups, LANES), AXES, 0, 0, t...]
    convert_element_type x4 -> x3, other arithmetic: 4.25 us -> 2.74 us  [split(): return (top.astype(bf16), (values - top).astype(bf16))]
    pallas_call x1, Pallas kernels: 14.1 us -> 12.7 us  [on_device(): pl.pallas_call(functools.partial(middle_kernel, unitary), out_shape=jax.S...]
    reshape x1 -> x0, local copies, waits for them, and re-layouts: 1.46 us -> none  [on_device(): high_term = got[:, :step].reshape(levels, groups, LANES).transpose(1, 2, 0)]
  transfers between devices with their start and end apart: 1 -> 1, of which waited for: 1 -> 1; matrix products, arithmetic and copies ran while one was open for 11% -> 12% of each run, Pallas kernels for 0% -> 0%
where the time goes in v1:
time: 104 us; the launch traced here: 103 us
  Pallas kernels  29.8 us (29%)
  blocking collectives  27.8 us (27%)
  waiting for transfers between devices  20.8 us (20%)
  starting transfers between devices  11.9 us (11%)
  other arithmetic  10.2 us (10%)
  local copies, waits for them, and re-layouts  1.97 us (2%)
    all_to_all x1, blocking collectives, on_device(): lax.all_to_all(sent.reshape(devices, step + groups, LANES), AXES, 0, 0, t...  27.8 us
    all_to_all x1, waiting for transfers between devices, on_device(): got = lax.all_to_all(sent, AXES, 0, 0, tiled=True)  20.8 us
    pallas_call x1, Pallas kernels, on_device(): pl.pallas_call(functools.partial(middle_kernel, unitary), out_shape=jax.S...  12.7 us
    all_to_all x1, starting transfers between devices, on_device(): got = lax.all_to_all(sent, AXES, 0, 0, tiled=True)  11.9 us
    pallas_call x1, Pallas kernels, on_device(): pl.pallas_call(finish_kernel, out_shape=(jax.ShapeDtypeStruct((groups, LA...  11.8 us
    pallas_call x1, Pallas kernels, on_device(): pl.pallas_call(prepare_kernel, out_shape=jax.ShapeDtypeStruct((devices, 2...  5.28 us
    select_n x2, other arithmetic, axis_table(): return jnp.where((index <= KL)[:, None], jnp.cos(angles), jnp.sin(angles))  4.58 us
    convert_element_type x3, other arithmetic, split(): return (top.astype(bf16), (values - top).astype(bf16))  2.74 us
  transfers between devices with their start and end apart: 1, of which 1 were waited for; matrix products, arithmetic and copies ran while one was open for 12% of the time, Pallas kernels for 0%

profile of v1, /device:TPU:1, one launch (start us, length us, event | category | flops | bytes accessed | tf_op | source)
XLA Modules:
  0.0 103.4 jit_solution(13931601105869449826)
XLA Ops:
  0.6 5.3 %prepare.1 = bf16[128,72,128]{2,1,0:T(8,128)(2,1)} custom-call(bf16[8,128,512]{2,1,0:T(8,128)(2,1)} %bitcast.10, bf16[8,128,512]{2,1,0:T(8,128)(2,1)} %bitcast.11, bf16[16,512]{1,0:T(8,128)(2,1)} %low_u_ref.1, bf16[16,512]{1,0:T(8,128)(2,1)} %low_v_ref.1, s32[16]{0:T(128)} %kx_ref.1, s32[16]{0:T(128)} %kz_ref.1), custom_call_target="tpu_custom_call" | custom-call | tf_op jit(solution)/shard_map/prepare/pallas_call | solution.py:512
  5.9 11.9 %all-to-all-start = ((bf16[128,72,128]{2,1,0:T(8,128)(2,1)}), bf16[128,72,128]{2,1,0:T(8,128)(2,1)}, u32[]{:S(2)}, u32[]{:S(2)}) async-start(bf16[128,72,128]{2,1,0:T(8,128)(2,1)} %prepare.1), calls=%async_computation | async-start | bytes 4718592 | tf_op jit(solution)/shard_map/all_to_all | solution.py:541
  17.9 0.1 broadcast_add_fusion
  18.0 0.1 add.202
  18.1 2.1 %sine_select_fusion = f32[2048,64]{0,1:T(8,128)S(1)} fusion(s32[2048]{0:T(1024)S(1)} %fusion.24, s32[64]{0:T(128)S(1)} %add_select_fusion.8, pred[64]{0:T(512)(128)(4,1)S(1)} %fusion.27), kind=kLoop, calls=%fused_computation.21 | loop fusion | flops 1966080 | bytes 532800 | tf_op jit(solution)/shard_map/jit(_where)/select_n | solution.py:28
  20.3 0.2 broadcast_select_fusion
  20.5 1.9 %copy.9 = f32[2048,256]{1,0:T(8,128)} copy(f32[2048,256]{0,1:T(8,128)S(1)} %bitcast.7) | data formatting | bytes 4194304 | tf_op jit(solution)/shard_map/jit(_where)/select_n | solution.py:68
  22.4 0.0 copy-start
  22.4 0.4 reduce-precision_convert_fusion.2
  22.8 0.6 pad_maximum_fusion.1.x_hbm
  23.4 0.6 reduce-precision_convert_fusion.1
  24.0 0.8 pad_maximum_fusion.back_x_hbm
  24.8 2.4 %sine_select_fusion.1 = bf16[64,2048]{1,0:T(8,128)(2,1)S(1)} fusion(s32[2048]{0:T(1024)S(1)} %fusion.24, s32[64]{0:T(128)S(1)} %add_select_fusion.8, pred[64]{0:T(512)(128)(4,1)S(1)} %fusion.27), kind=kLoop, calls=%fused_computation.22 | loop fusion | flops 1966080 | bytes 270656 | tf_op jit(solution)/shard_map/jit(_where)/select_n | solution.py:28
  27.3 1.2 %select_convert_fusion = bf16[4,64,2048]{2,1,0:T(8,128)(2,1)} fusion(bf16[64,2048]{1,0:T(8,128)(2,1)S(1)} %sine_select_fusion.1, pred[4,2048]{1,0:T(4,128)(4,1)S(1)} %iota_compare_fusion.1), kind=kLoop, calls=%fused_computation.3 | loop fusion | flops 524288 | bytes 1318912 | tf_op jit(solution)/shard_map/convert_element_type | solution.py:72
  28.4 0.0 copy-done
  28.4 1.7 %fusion = (bf16[2048,256]{1,0:T(8,128)(2,1)}, bf16[2048,256]{1,0:T(8,128)(2,1)}) fusion(f32[2048,256]{1,0:T(8,128)S(1)} %copy-done), kind=kLoop, calls=%fused_computation.2 | loop fusion | flops 2097152 | bytes 4194304 | tf_op jit(solution)/shard_map/convert_element_type | solution.py:33
  30.2 20.8 %all-to-all-done = bf16[128,72,128]{2,1,0:T(8,128)(2,1)} async-done(((bf16[128,72,128]{2,1,0:T(8,128)(2,1)}), bf16[128,72,128]{2,1,0:T(8,128)(2,1)}, u32[]{:S(2)}, u32[]{:S(2)}) %all-to-all-start) | async-done | bytes 2359328 | tf_op jit(solution)/shard_map/all_to_all | solution.py:541
  51.0 12.7 %middle.1 = bf16[8,16,40,128]{3,2,1,0:T(8,128)(2,1)} custom-call(bf16[8,16,72,128]{3,2,1,0:T(8,128)(2,1)} %bitcast.2.got_hbm, bf16[256,160]{1,0:T(8,128)(2,1)} %pad_maximum_fusion.back_x_hbm, bf16[160,256]{1,0:T(8,128)(2,1)} %pad_maximum_fusion.1.x_hbm, bf16[256,2048]{1,0:T(8,128)(2,1)} %bitcast.9, bf16[2048,256]{1,0:T(8,128)(2,1)} %get-tuple-element.7.z_top_hbm, ...), custom_call_target="tpu_custom_call" | custom-call | tf_op jit(solution)/shard_map/middle/pallas_call | solution.py:545
  63.6 27.8 %all_to_all.10.got_hbm = bf16[128,40,128]{2,1,0:T(8,128)(2,1)} all-to-all(bf16[128,40,128]{2,1,0:T(8,128)(2,1)} %bitcast.8), channel_id=1, replica_groups=mesh['gx'=8,'gz'=16] {'gx','gz'}, dimensions={0} | all-to-all | bytes 2621440 | tf_op jit(solution)/shard_map/all_to_all | solution.py:583
  91.4 11.8 %finish.1 = (bf16[8,128,512]{2,1,0:T(8,128)(2,1)}, f32[16,512]{1,0:T(8,128)}) custom-call(bf16[128,40,128]{2,1,0:T(8,128)(2,1)} %all_to_all.10.got_hbm, bf16[16,512,512]{2,1,0:T(8,128)(2,1)} %tau_hbm.1), custom_call_target="tpu_custom_call" | custom-call | tf_op jit(solution)/shard_map/finish/pallas_call | solution.py:587
  (10 shorter events, 0.1 us)
Async XLA Ops:
  5.9 45.0 %all-to-all-start = ((bf16[128,72,128]{2,1,0:T(8,128)(2,1)}), bf16[128,72,128]{2,1,0:T(8,128)(2,1)}, u32[]{:S(2)}, u32[]{:S(2)}) async-start(bf16[128,72,128]{2,1,0:T(8,128)(2,1)} %prepare.1), calls=%async_computation | async-start | bytes 4718592 | tf_op jit(solution)/shard_map/all_to_all | solution.py:541
  22.4 6.1 %copy-start = (f32[2048,256]{1,0:T(8,128)S(1)}, f32[2048,256]{1,0:T(8,128)}, u32[]{:S(2)}) copy-start(f32[2048,256]{1,0:T(8,128)} %copy.9) | copy-start | bytes 6291460

commit v2 on v1

--- a/solution.py
+++ b/solution.py
@@ -16,7 +16,6 @@
 AXES = ("gx", "gz")
 INTERPRET = False
 WHOLE = 67043328
-UNROLL = 1
 bf16 = jnp.bfloat16
 f32 = jnp.float32
 
@@ -133,41 +132,74 @@
         return pltpu.make_async_copy(ready.at[part], out_ref.at[part], out_sem.at[k])
 
     lane = lax.broadcasted_iota(jnp.int32, (1, LANES), 1)
-    line = jnp.zeros((1, LANES), f32)
-    for m in range(owned):
+
+    def place(m, line):
         line = jnp.where(lane == owned + m, index[0, m].astype(f32), line)
-        line = jnp.where(lane == 2 * owned + m, index[1, m].astype(f32), line)
-    eye = identity(LANES)
-    for k in range(2):
+        return jnp.where(lane == 2 * owned + m, index[1, m].astype(f32), line)
+
+    line = lax.fori_loop(0, owned, place, jnp.zeros((1, LANES), f32))
+
+    def lower(k, _):
         padded = jnp.concatenate(
             [lows[k].astype(f32), jnp.zeros((LANES - owned, levels), f32)], axis=0
         ).astype(bf16)
-        for y in range(0, levels, LANES):
-            low[pl.ds(y, LANES), :] = across(eye, padded[:, y : y + LANES])
+        low[...] = jnp.concatenate(
+            [
+                across(identity(LANES), padded[:, y : y + LANES])
+                for y in range(0, levels, LANES)
+            ],
+            axis=0,
+        )
         for y in range(rows):
             tile[pl.ds(k * rows + y, devices, stride=groups), :] = (
                 low[pl.ds(y, devices, stride=rows), :] + line
             )
-    ready[:, 2 * step :, :] = tile[...].astype(bf16).reshape(devices, groups, LANES)
-    sends = [send(2, 2 * step, groups)]
-    sends[0].start()
-    eye = identity(side)
-    for k in range(2):
-        for g in range(pairs):
-            copies[4 + k * pairs + g].wait()
-            block = fine[k, 2 * g : 2 * g + 2].reshape(side, levels)
+        return 0
+
+    lax.fori_loop(0, 2, lower, 0)
+    block = 16
+
+    def round_tile(b, _):
+        at = pl.ds(pl.multiple_of(b * block * groups, block * groups), block * groups)
+        ready[pl.ds(b * block, block), 2 * step :, :] = (
+            tile[at, :].astype(bf16).reshape(block, groups, LANES)
+        )
+        return 0
+
+    lax.fori_loop(0, devices // block, round_tile, 0)
+    send(2, 2 * step, groups).start()
+
+    def turn(k, _):
+        def turn_pair(g, _):
+            pltpu.make_async_copy(
+                u_ref.at[pl.ds(0, 2)], fine.at[k, pl.ds(2 * g, 2)], fine_sem.at[k, g]
+            ).wait()
+            part = fine[k, pl.ds(2 * g, 2)].reshape(side, levels)
             for y in range(0, levels, side):
-                turned = across(eye, block[:, y : y + side])
+                turned = across(identity(side), part[:, y : y + side])
                 at = y * groups + 2 * g
                 tall[pl.ds(at, side, stride=groups), :] = turned[:, :LANES]
                 tall[pl.ds(at + 1, side, stride=groups), :] = turned[:, LANES:]
-        ready[:, k * step : (k + 1) * step, :] = (
-            tall[...].astype(bf16).reshape(devices, step, LANES)
-        )
-        sends.append(send(k, k * step, step))
-        sends[-1].start()
-    for copy in sends:
-        copy.wait()
+            return 0
+
+        lax.fori_loop(0, pairs, turn_pair, 0)
+        first = pl.multiple_of(k * step, step)
+
+        def round_lines(b, _):
+            at = pl.ds(pl.multiple_of(b * block * step, block * step), block * step)
+            ready[pl.ds(b * block, block), pl.ds(first, step), :] = (
+                tall[at, :].astype(bf16).reshape(block, step, LANES)
+            )
+            return 0
+
+        lax.fori_loop(0, devices // block, round_lines, 0)
+        send(k, first, step).start()
+        return 0
+
+    lax.fori_loop(0, 2, turn, 0)
+    send(2, 2 * step, groups).wait()
+    for k in range(2):
+        send(k, k * step, step).wait()
 
 
 def middle_kernel(
@@ -187,16 +219,19 @@
     z_rest_ref,
     out_ref,
     modes,
+    turned,
     left,
     right,
+    hits,
+    table,
     spectrum,
     wave,
     mean,
     wave_top,
-    products,
     sums,
     cross,
     coefficients,
+    force,
     picked,
     in_sem,
     out_sem,
@@ -234,64 +269,86 @@
     for fetch in fetches:
         fetch.start()
     fetches[0].wait()
-    modes[...] = got_ref[:, :, 2 * step :, :].astype(f32).reshape(devices * groups, LANES)
-    first = modes[pl.ds(0, devices, stride=groups), :]
-    turned = [first.T]
-    for c in range(1, 2 * rows):
-        turned.append(modes[pl.ds(c, devices, stride=groups), :].T)
+    def widen(i, _):
+        at = pl.ds(pl.multiple_of(i * LANES, LANES), LANES)
+        modes[at, :] = got_ref[i, :, 2 * step :, :].astype(f32).reshape(LANES, LANES)
+        return 0
+
+    lax.fori_loop(0, groups_x, widen, 0)
+
+    def turn(c, _):
+        turned[c] = modes[pl.ds(c, devices, stride=groups), :].T
+        return 0
+
+    lax.fori_loop(0, 2 * rows, turn, 0)
     row = lax.broadcasted_iota(jnp.int32, (PADDED, devices), 0).astype(f32)
-    column = lax.broadcasted_iota(jnp.int32, (devices, LANES), 1)
-    wanted = (1 + column % HALF).astype(f32)
-    for m in range(owned):
-        at = slice(m * devices, (m + 1) * devices)
-        hit = row == turned[0][owned + m : owned + m + 1, :]
-        hit = jnp.where(hit, 1.0, 0.0).astype(bf16)
-        for c in range(2 * rows):
-            value = jnp.broadcast_to(turned[c][m : m + 1, :], (16, devices)).astype(bf16)
-            value = jnp.concatenate([value] * (PADDED // 16), axis=0)
-            left[c * PADDED : (c + 1) * PADDED, at] = hit * value
-        left[2 * rows * PADDED :, at] = hit
-        index_z = jnp.broadcast_to(
-            first[:, 2 * owned + m : 2 * owned + m + 1], (devices, LANES)
+    wanted = lax.broadcasted_iota(jnp.int32, (LANES, devices), 0)
+    wanted = (1 + wanted % HALF).astype(f32)
+    table[...] = jnp.zeros_like(table)
+
+    def gather(p, _):
+        for e in range(2):
+            m = 2 * p + e
+            at = slice(e * devices, (e + 1) * devices)
+            hit = row == turned[0, pl.ds(owned + m, 1), :]
+            hit = jnp.where(hit, 1.0, 0.0).astype(bf16)
+            for c in range(2 * rows):
+                value = jnp.broadcast_to(turned[c, pl.ds(m, 1), :], (16, devices))
+                value = jnp.concatenate([value.astype(bf16)] * (PADDED // 16), axis=0)
+                left[c * PADDED : (c + 1) * PADDED, at] = hit * value
+            left[2 * rows * PADDED :, at] = hit
+            hits[:, pl.ds(pl.multiple_of(m * devices, devices), devices)] = hit
+            index_z = turned[0, pl.ds(2 * owned + m, 1), :]
+            right[:LANES, at] = jnp.where(wanted == index_z, 1.0, 0.0).astype(bf16)
+            right[LANES:, at] = jnp.broadcast_to(
+                jnp.where(index_z == 0.0, 1.0, 0.0), (LANES, devices)
+            ).astype(bf16)
+        table[...] += across(left[...], right[...])
+        return 0
+
+    lax.fori_loop(0, owned // 2, gather, 0)
+
+    def round_table(c, _):
+        at = pl.ds(pl.multiple_of(c * PADDED, PADDED), PADDED)
+        spectrum[at, :] = table[at, :].astype(bf16)
+        return 0
+
+    lax.fori_loop(0, 2 * rows + 1, round_table, 0)
+    fetches[1].wait()
+
+    def spread(k, y, part):
+        full = dot(back_x_ref[...], jnp.concatenate([part, part], axis=0))
+        part = [full[p * points : (p + 1) * points] for p in range(4)]
+        waves = jnp.concatenate(
+            [
+                jnp.where(low_half, part[0][:, :LANES], part[1][:, :LANES]),
+                jnp.where(low_half, part[2][:, :LANES], part[3][:, :LANES]),
+            ],
+            axis=1,
         )
-        right[at, :LANES] = jnp.where(wanted == index_z, 1.0, 0.0).astype(bf16)
-        right[at, LANES:] = jnp.where(index_z == 0.0, 1.0, 0.0).astype(bf16)
-    spectrum[...] = dot(left[...], right[...]).astype(bf16)
-    fetches[1].wait()
-
-    def spread(k, parts):
-        both = jnp.concatenate(parts, axis=1)
-        full = dot(back_x_ref[...], jnp.concatenate([both, both], axis=0))
-        for y in range(len(parts)):
-            part = [
-                full[p * points : (p + 1) * points, y * side : (y + 1) * side]
-                for p in range(4)
-            ]
-            waves = jnp.concatenate(
-                [
-                    jnp.where(low_half, part[0][:, :LANES], part[1][:, :LANES]),
-                    jnp.where(low_half, part[2][:, :LANES], part[3][:, :LANES]),
-                ],
-                axis=1,
-            )
-            constant = part[3][:, LANES:]
-            for p in range(3):
-                constant = jnp.where(which == p, part[p][:, LANES:], constant)
-            wave[k, :, y] = waves.reshape(groups_x, groups, side)
-            mean[k, :, y] = constant.reshape(groups_x, groups, LANES)
-
-    for k in range(2):
-        spread(
-            k,
-            [
-                spectrum[(k * rows + y) * PADDED : (k * rows + y + 1) * PADDED, :]
-                for y in range(rows)
-            ],
-        )
-    wave_top[...] = wave[...].reshape(2 * half_rows, side).astype(bf16)
+        constant = part[3][:, LANES:]
+        for p in range(3):
+            constant = jnp.where(which == p, part[p][:, LANES:], constant)
+        wave[k, :, y] = waves.reshape(groups_x, groups, side)
+        mean[k, :, y] = constant.reshape(groups_x, groups, LANES)
+
+    def spread_low(c, _):
+        at = pl.ds(pl.multiple_of(c * PADDED, PADDED), PADDED)
+        spread(c // rows, c % rows, spectrum[at, :])
+        return 0
+
+    lax.fori_loop(0, 2 * rows, spread_low, 0)
+
+    def round_wave(k, _):
+        at = pl.ds(pl.multiple_of(k * half_rows, half_rows), half_rows)
+        wave_top[at, :] = wave[k].reshape(half_rows, side).astype(bf16)
+        return 0
+
+    lax.fori_loop(0, 2, round_wave, 0)
     sums[...] = jnp.zeros_like(sums)
-    fetches[2].wait()
-    fetches[3].wait()
+    coefficients[...] = jnp.zeros_like(coefficients)
+    for fetch in fetches[2:]:
+        fetch.wait()
 
     def fine(j, k):
         parts = [
@@ -311,87 +368,98 @@
         cross_term = coarse_u * fine_v + fine_u * coarse_v
         cross[:, at] = cross_term
         cross_round = cross_term.astype(bf16)
-        products[:half_rows, at] = self_term
-        products[half_rows:, at] = cross_round
         for k, term in enumerate((self_term, cross_round)):
             wide = term.astype(f32)
             sums[k] += (wide[:, :LANES] + wide[:, LANES:]).reshape(
                 groups_x, rows, groups, LANES
             )
-        return 0
-
-    lax.fori_loop(0, groups_z // 2, multiply, 0, unroll=UNROLL)
-    for fetch in fetches[4:]:
-        fetch.wait()
-    both = dot(products[...], z_top_ref[...]) + dot(products[...], z_rest_ref[...])
-    coefficients[...] = both.reshape(2, groups_x, rows, groups, side)
-
-    def project(k):
-        stacks = []
-        for y in range(rows):
-            waves = coefficients[k, :, y].reshape(points, side)
-            total = sums[k, :, y].reshape(points, LANES)
-            stack = []
-            for part in range(4):
-                half = waves[:, :LANES] if part < 2 else waves[:, LANES:]
-                keep = low_half if part % 2 == 0 else jnp.logical_not(low_half)
-                stack.append(
-                    jnp.concatenate(
-                        [
-                            jnp.where(keep, half, 0.0),
-                            jnp.where(which == part, total, 0.0),
-                        ],
-                        axis=1,
-                    )
+            share = dot(term, z_top_ref[at, :]) + dot(term, z_rest_ref[at, :])
+            coefficients[k] += share.reshape(groups_x, rows, groups, side)
+        return 0
+
+    lax.fori_loop(0, groups_z // 2, multiply, 0)
+
+    def project(k, y):
+        waves = coefficients[k, :, y].reshape(points, side)
+        total = sums[k, :, y].reshape(points, LANES)
+        stack = []
+        for part in range(4):
+            half = waves[:, :LANES] if part < 2 else waves[:, LANES:]
+            keep = low_half if part % 2 == 0 else jnp.logical_not(low_half)
+            stack.append(
+                jnp.concatenate(
+                    [
+                        jnp.where(keep, half, 0.0),
+                        jnp.where(which == part, total, 0.0),
+                    ],
+                    axis=1,
                 )
-            stacks.append(jnp.concatenate(stack, axis=0))
-        top, rest = halves(jnp.concatenate(stacks, axis=1))
+            )
+        top, rest = halves(jnp.concatenate(stack, axis=0))
         outer = dot(x_ref[...], top)
         outer = outer[:PADDED] + outer[PADDED:] + dot(x_ref[:PADDED], rest)
-        done = []
-        for y in range(rows):
-            waves = outer[:, y * side : y * side + LANES] * unitary
-            waves = waves + pltpu.roll(waves, HALF, 1)
-            constant = outer[:, y * side + LANES : (y + 1) * side]
-            constant = jnp.sum(constant, axis=1, keepdims=True) * unitary
-            done.append((waves, jnp.broadcast_to(constant, (PADDED, LANES))))
-        return done
+        waves = outer[:, :LANES] * unitary
+        waves = waves + pltpu.roll(waves, HALF, 1)
+        constant = jnp.sum(outer[:, LANES:], axis=1, keepdims=True) * unitary
+        return waves, jnp.broadcast_to(constant, (PADDED, LANES))
 
     row_index = lax.broadcasted_iota(jnp.int32, (PADDED, 1), 0)
     weight_x = jnp.where(row_index > 0, 2.0, 1.0).astype(f32)
-    mask = spectrum[2 * rows * PADDED :, :]
-    parts = []
-    for waves, constant in project(1):
+
+    def restore(y, _):
+        waves, constant = project(1, y)
         low = jnp.concatenate([waves * (2.0 * weight_x), constant * weight_x], axis=1)
-        parts.append(low.astype(bf16) * mask)
-    spread(0, parts)
-    wave_top[:half_rows] = wave[0].reshape(half_rows, side).astype(bf16)
-
-    kept = 72
-    parts = []
-    for waves, constant in project(0):
-        force = jnp.where(low_half, waves, jnp.where(lane == HALF, constant, 0.0))
-        force = jnp.concatenate([force, jnp.zeros((LANES - PADDED, LANES), f32)], axis=0)
-        parts.append(force.T[:kept])
-    force = jnp.concatenate(parts, axis=0).astype(bf16)[:, :PADDED]
-    line = lax.broadcasted_iota(jnp.int32, (kept, devices), 0)
+        spread(0, y, low.astype(bf16) * spectrum[2 * rows * PADDED :, :])
+        return 0
+
+    lax.fori_loop(0, rows, restore, 0)
+    lax.fori_loop(0, 1, round_wave, 0)
+
+    def push(y, _):
+        waves, constant = project(0, y)
+        value = jnp.where(low_half, waves, jnp.where(lane == HALF, constant, 0.0))
+        value = jnp.concatenate([value, jnp.zeros((LANES - PADDED, LANES), f32)], axis=0)
+        force[y] = value.T[:PADDED]
+        return 0
+
+    lax.fori_loop(0, rows, push, 0)
+    line = lax.broadcasted_iota(jnp.int32, (PADDED, devices), 0)
     line = jnp.where(line < HALF, line + 1, jnp.where(line == HALF, 0, -1)).astype(f32)
     picked[...] = jnp.zeros_like(picked)
-    for m in range(0, owned, 2):
-        chosen = dot(force, left[2 * rows * PADDED :, m * devices : (m + 2) * devices])
+
+    def pick(p, _):
+        at = pl.ds(pl.multiple_of(p * 2 * devices, 2 * devices), 2 * devices)
+        values = force[...].reshape(rows * PADDED, LANES).astype(bf16)[:, :PADDED]
+        chosen = dot(values, hits[:, at])
         for e in range(2):
-            hit = line == turned[0][2 * owned + m + e : 2 * owned + m + e + 1, :]
+            m = 2 * p + e
+            hit = line == turned[0, pl.ds(2 * owned + m, 1), :]
             for y in range(rows):
-                value = chosen[y * kept : (y + 1) * kept, e * devices : (e + 1) * devices]
-                picked[y, m + e : m + e + 1, :] = jnp.sum(
+                value = chosen[
+                    y * PADDED : (y + 1) * PADDED, e * devices : (e + 1) * devices
+                ]
+                picked[y, pl.ds(m, 1), :] = jnp.sum(
                     jnp.where(hit, value, 0.0), axis=0, keepdims=True
                 )
+        return 0
+
+    lax.fori_loop(0, owned // 2, pick, 0)
     modes[...] = jnp.zeros_like(modes)
-    for y in range(rows):
+
+    def turn_back(y, _):
         modes[pl.ds(y, devices, stride=groups), :] = picked[y].T
-    out_ref[:, :, step:, :] = (
-        modes[...].astype(bf16).reshape(groups_x, groups_z, groups, LANES)
-    )
+        return 0
+
+    lax.fori_loop(0, rows, turn_back, 0)
+
+    def narrow(i, _):
+        at = pl.ds(pl.multiple_of(i * LANES, LANES), LANES)
+        out_ref[i, :, step:, :] = modes[at, :].astype(bf16).reshape(
+            groups_z, groups, LANES
+        )
+        return 0
+
+    lax.fori_loop(0, groups_x, narrow, 0)
     part = everything + (pl.ds(step, groups),)
     send_tiles = pltpu.make_async_copy(
         out_ref.at[part], out_hbm.at[part], out_sem.at[groups_z // 2]
@@ -415,7 +483,7 @@
         send(j).start()
         return 0
 
-    lax.fori_loop(0, groups_z // 2, subtract, 0, unroll=UNROLL)
+    lax.fori_loop(0, groups_z // 2, subtract, 0)
     send_tiles.wait()
 
     def drain(j, _):
@@ -435,6 +503,7 @@
     tall,
     tile,
     force,
+    vector,
     ready,
     got_sem,
     tau_sem,
@@ -459,35 +528,43 @@
         )
     for fetch in fetches:
         fetch.start()
-    eye = identity(LANES)
-    sends = []
-    for q in range(count):
-        fetches[q].wait()
-        at = slice(q * chunk, (q + 1) * chunk)
+    def send(q):
+        part = (slice(None), slice(None), pl.ds(pl.multiple_of(q * LANES, LANES), LANES))
+        return pltpu.make_async_copy(ready.at[part], high_hbm.at[part], out_sem.at[q])
+
+    def turn(q, _):
+        at = pl.ds(q * chunk, chunk)
+        pltpu.make_async_copy(got_hbm.at[at], got_ref.at[at], got_sem.at[q]).wait()
         tall[...] = got_ref[at, :step, :].astype(f32).reshape(chunk * step, LANES)
-        where = pl.ds(q * LANES, LANES)
+        where = pl.ds(pl.multiple_of(q * LANES, LANES), LANES)
         for g in range(groups):
             column = tall[pl.ds(g, LANES, stride=groups), :].astype(bf16)
-            ready[g, :, q * LANES : (q + 1) * LANES] = across(eye, column).astype(bf16)
-        part = (slice(None), slice(None), where)
-        sends.append(
-            pltpu.make_async_copy(ready.at[part], high_hbm.at[part], out_sem.at[q])
-        )
-        sends[-1].start()
+            ready[g, :, where] = across(identity(LANES), column).astype(bf16)
+        send(q).start()
+        return 0
+
+    lax.fori_loop(0, count, turn, 0)
     tile[...] = got_ref[:, step:, :].astype(f32).reshape(devices * groups, LANES)
     for y in range(rows):
         force[pl.ds(y, devices, stride=rows), :] = tile[
             pl.ds(y, devices, stride=groups), :
         ]
-    vector = force[...].astype(bf16)
-    lane = lax.broadcasted_iota(jnp.int32, (levels, LANES), 1)
-    answer = jnp.zeros((levels, LANES), f32)
-    for m in range(owned):
-        fetches[count + m].wait()
-        answer = jnp.where(lane == m, dot(tau_ref[m], vector), answer)
-    low_ref[...] = answer.T[:owned]
-    for copy in sends:
-        copy.wait()
+    vector[...] = force[...].astype(bf16)
+    lane = lax.broadcasted_iota(jnp.int32, (1, LANES), 1)
+
+    def solve(m, _):
+        pltpu.make_async_copy(tau_hbm.at[m], tau_ref.at[m], tau_sem.at[m]).wait()
+        force[...] = jnp.where(lane == m, dot(tau_ref[m], vector[...]), force[...])
+        return 0
+
+    lax.fori_loop(0, owned, solve, 0)
+    low_ref[...] = force[...].T[:owned]
+
+    def drain(q, _):
+        send(q).wait()
+        return 0
+
+    lax.fori_loop(0, count, drain, 0)
 
 
 def on_device(high_u, high_v, low_u, low_v, low_kx, low_kz, tau_inverse):
@@ -556,16 +633,19 @@
             pltpu.VMEM(forward_z[1].shape, bf16),
             pltpu.VMEM((groups_x, groups_z, step + groups, LANES), bf16),
             pltpu.VMEM((devices * groups, LANES), f32),
-            pltpu.VMEM(((2 * rows + 1) * PADDED, owned * devices), bf16),
-            pltpu.VMEM((owned * devices, side), bf16),
+            pltpu.VMEM((2 * rows, LANES, devices), f32),
+            pltpu.VMEM(((2 * rows + 1) * PADDED, 2 * devices), bf16),
+            pltpu.VMEM((side, 2 * devices), bf16),
+            pltpu.VMEM((PADDED, owned * devices), bf16),
+            pltpu.VMEM(((2 * rows + 1) * PADDED, side), f32),
             pltpu.VMEM(((2 * rows + 1) * PADDED, side), bf16),
             pltpu.VMEM((2, groups_x, rows, groups, side), f32),
             pltpu.VMEM((2, groups_x, rows, groups, LANES), f32),
             pltpu.VMEM((2 * half_rows, side), bf16),
-            pltpu.VMEM((2 * half_rows, width), bf16),
             pltpu.VMEM((2, groups_x, rows, groups, LANES), f32),
             pltpu.VMEM((half_rows, width), f32),
             pltpu.VMEM((2, groups_x, rows, groups, side), f32),
+            pltpu.VMEM((rows, PADDED, LANES), f32),
             pltpu.VMEM((rows, LANES, devices), f32),
             pltpu.SemaphoreType.DMA((7,)),
             pltpu.SemaphoreType.DMA((groups_z // 2 + 1,)),
@@ -598,6 +678,7 @@
             pltpu.VMEM((LANES * groups, LANES), f32),
             pltpu.VMEM((devices * groups, LANES), f32),
             pltpu.VMEM((levels, LANES), f32),
+            pltpu.VMEM((levels, LANES), bf16),
             pltpu.VMEM((groups, LANES, levels), bf16),
             pltpu.SemaphoreType.DMA((devices * rows // LANES,)),
             pltpu.SemaphoreType.DMA((owned,)),

time: 104 us -> 107 us (1.029)
  Pallas kernels: 29.8 us -> 33.7 us
    pallas_call x1, Pallas kernels: 12.7 us -> 18.1 us  [on_device(): pl.pallas_call(functools.partial(middle_kernel, unitary), out_shape=jax.S...]
    pallas_call x1, Pallas kernels: 11.8 us -> 9.96 us  [on_device(): pl.pallas_call(finish_kernel, out_shape=(jax.ShapeDtypeStruct((groups, LA...]
  transfers between devices with their start and end apart: 1 -> 1, of which waited for: 1 -> 1; matrix products, arithmetic and copies ran while one was open for 12% -> 11% of each run, Pallas kernels for 0% -> 0%
where the time goes in v2:
time: 107 us
  Pallas kernels  33.7 us (31%)
  blocking collectives  27.8 us (26%)
  waiting for transfers between devices  20.8 us (19%)
  starting transfers between devices  11.9 us (11%)
  other arithmetic  10.2 us (10%)
  local copies, waits for them, and re-layouts  1.97 us (2%)
    all_to_all x1, blocking collectives, on_device(): lax.all_to_all(sent.reshape(devices, step + groups, LANES), AXES, 0, 0, t...  27.8 us
    all_to_all x1, waiting for transfers between devices, on_device(): got = lax.all_to_all(sent, AXES, 0, 0, tiled=True)  20.8 us
    pallas_call x1, Pallas kernels, on_device(): pl.pallas_call(functools.partial(middle_kernel, unitary), out_shape=jax.S...  18.1 us
    all_to_all x1, starting transfers between devices, on_device(): got = lax.all_to_all(sent, AXES, 0, 0, tiled=True)  11.9 us
    pallas_call x1, Pallas kernels, on_device(): pl.pallas_call(finish_kernel, out_shape=(jax.ShapeDtypeStruct((groups, LA...  9.96 us
    pallas_call x1, Pallas kernels, on_device(): pl.pallas_call(prepare_kernel, out_shape=jax.ShapeDtypeStruct((devices, 2...  5.65 us
    select_n x2, other arithmetic, axis_table(): return jnp.where((index <= KL)[:, None], jnp.cos(angles), jnp.sin(angles))  4.58 us
    convert_element_type x3, other arithmetic, split(): return (top.astype(bf16), (values - top).astype(bf16))  2.74 us
  transfers between devices with their start and end apart: 1, of which 1 were waited for; matrix products, arithmetic and copies ran while one was open for 11% of the time, Pallas kernels for 0%

profile of v2, /device:TPU:1, one launch (start us, length us, event | category | flops | bytes accessed | tf_op | source)
XLA Modules:
  0.0 107.2 jit_solution(16050803016606972513)
XLA Ops:
  0.6 5.6 %prepare.1 = bf16[128,72,128]{2,1,0:T(8,128)(2,1)} custom-call(bf16[8,128,512]{2,1,0:T(8,128)(2,1)} %bitcast.10, bf16[8,128,512]{2,1,0:T(8,128)(2,1)} %bitcast.11, bf16[16,512]{1,0:T(8,128)(2,1)} %low_u_ref.1, bf16[16,512]{1,0:T(8,128)(2,1)} %low_v_ref.1, s32[16]{0:T(128)} %kx_ref.1, s32[16]{0:T(128)} %kz_ref.1), custom_call_target="tpu_custom_call" | custom-call | tf_op jit(solution)/shard_map/prepare/pallas_call | solution.py:589
  6.3 11.9 %all-to-all-start = ((bf16[128,72,128]{2,1,0:T(8,128)(2,1)}), bf16[128,72,128]{2,1,0:T(8,128)(2,1)}, u32[]{:S(2)}, u32[]{:S(2)}) async-start(bf16[128,72,128]{2,1,0:T(8,128)(2,1)} %prepare.1), calls=%async_computation | async-start | bytes 4718592 | tf_op jit(solution)/shard_map/all_to_all | solution.py:618
  18.3 0.1 broadcast_add_fusion
  18.3 0.1 add.202
  18.5 2.1 %sine_select_fusion = f32[2048,64]{0,1:T(8,128)S(1)} fusion(s32[2048]{0:T(1024)S(1)} %fusion.24, s32[64]{0:T(128)S(1)} %add_select_fusion.8, pred[64]{0:T(512)(128)(4,1)S(1)} %fusion.27), kind=kLoop, calls=%fused_computation.21 | loop fusion | flops 1966080 | bytes 532800 | tf_op jit(solution)/shard_map/jit(_where)/select_n | solution.py:27
  20.6 0.2 broadcast_select_fusion
  20.8 1.9 %copy.9 = f32[2048,256]{1,0:T(8,128)} copy(f32[2048,256]{0,1:T(8,128)S(1)} %bitcast.7) | data formatting | bytes 4194304 | tf_op jit(solution)/shard_map/jit(_where)/select_n | solution.py:67
  22.7 0.0 copy-start
  22.7 0.4 reduce-precision_convert_fusion.2
  23.1 0.6 pad_maximum_fusion.1.x_hbm
  23.8 0.6 reduce-precision_convert_fusion.1
  24.4 0.8 pad_maximum_fusion.back_x_hbm
  25.2 2.4 %sine_select_fusion.1 = bf16[64,2048]{1,0:T(8,128)(2,1)S(1)} fusion(s32[2048]{0:T(1024)S(1)} %fusion.24, s32[64]{0:T(128)S(1)} %add_select_fusion.8, pred[64]{0:T(512)(128)(4,1)S(1)} %fusion.27), kind=kLoop, calls=%fused_computation.22 | loop fusion | flops 1966080 | bytes 270656 | tf_op jit(solution)/shard_map/jit(_where)/select_n | solution.py:27
  27.6 1.2 %select_convert_fusion = bf16[4,64,2048]{2,1,0:T(8,128)(2,1)} fusion(bf16[64,2048]{1,0:T(8,128)(2,1)S(1)} %sine_select_fusion.1, pred[4,2048]{1,0:T(4,128)(4,1)S(1)} %iota_compare_fusion.1), kind=kLoop, calls=%fused_computation.3 | loop fusion | flops 524288 | bytes 1318912 | tf_op jit(solution)/shard_map/convert_element_type | solution.py:71
  28.8 0.0 copy-done
  28.8 1.7 %fusion = (bf16[2048,256]{1,0:T(8,128)(2,1)}, bf16[2048,256]{1,0:T(8,128)(2,1)}) fusion(f32[2048,256]{1,0:T(8,128)S(1)} %copy-done), kind=kLoop, calls=%fused_computation.2 | loop fusion | flops 2097152 | bytes 4194304 | tf_op jit(solution)/shard_map/convert_element_type | solution.py:32
  30.5 20.8 %all-to-all-done = bf16[128,72,128]{2,1,0:T(8,128)(2,1)} async-done(((bf16[128,72,128]{2,1,0:T(8,128)(2,1)}), bf16[128,72,128]{2,1,0:T(8,128)(2,1)}, u32[]{:S(2)}, u32[]{:S(2)}) %all-to-all-start) | async-done | bytes 2359328 | tf_op jit(solution)/shard_map/all_to_all | solution.py:618
  51.3 18.1 %middle.1 = bf16[8,16,40,128]{3,2,1,0:T(8,128)(2,1)} custom-call(bf16[8,16,72,128]{3,2,1,0:T(8,128)(2,1)} %bitcast.2.got_hbm, bf16[256,160]{1,0:T(8,128)(2,1)} %pad_maximum_fusion.back_x_hbm, bf16[160,256]{1,0:T(8,128)(2,1)} %pad_maximum_fusion.1.x_hbm, bf16[256,2048]{1,0:T(8,128)(2,1)} %bitcast.9, bf16[2048,256]{1,0:T(8,128)(2,1)} %get-tuple-element.7.z_top_hbm, ...), custom_call_target="tpu_custom_call" | custom-call | tf_op jit(solution)/shard_map/middle/pallas_call | solution.py:622
  69.5 27.8 %all_to_all.10.got_hbm = bf16[128,40,128]{2,1,0:T(8,128)(2,1)} all-to-all(bf16[128,40,128]{2,1,0:T(8,128)(2,1)} %bitcast.8), channel_id=1, replica_groups=mesh['gx'=8,'gz'=16] {'gx','gz'}, dimensions={0} | all-to-all | bytes 2621440 | tf_op jit(solution)/shard_map/all_to_all | solution.py:663
  97.2 10.0 %finish.1 = (bf16[8,128,512]{2,1,0:T(8,128)(2,1)}, f32[16,512]{1,0:T(8,128)}) custom-call(bf16[128,40,128]{2,1,0:T(8,128)(2,1)} %all_to_all.10.got_hbm, bf16[16,512,512]{2,1,0:T(8,128)(2,1)} %tau_hbm.1), custom_call_target="tpu_custom_call" | custom-call | tf_op jit(solution)/shard_map/finish/pallas_call | solution.py:667
  (10 shorter events, 0.1 us)
Async XLA Ops:
  6.3 45.0 %all-to-all-start = ((bf16[128,72,128]{2,1,0:T(8,128)(2,1)}), bf16[128,72,128]{2,1,0:T(8,128)(2,1)}, u32[]{:S(2)}, u32[]{:S(2)}) async-start(bf16[128,72,128]{2,1,0:T(8,128)(2,1)} %prepare.1), calls=%async_computation | async-start | bytes 4718592 | tf_op jit(solution)/shard_map/all_to_all | solution.py:618
  22.7 6.1 %copy-start = (f32[2048,256]{1,0:T(8,128)S(1)}, f32[2048,256]{1,0:T(8,128)}, u32[]{:S(2)}) copy-start(f32[2048,256]{1,0:T(8,128)} %copy.9) | copy-start | bytes 6291460

commit v3 on v1

--- a/solution.py
+++ b/solution.py
@@ -15,8 +15,12 @@
 HALF = LANES // 2
 AXES = ("gx", "gz")
 INTERPRET = False
+MIB = 1024 * 1024
 WHOLE = 67043328
-UNROLL = 1
+PREPARE = WHOLE
+MIDDLE = 24 * MIB
+STAGE = 16 * MIB
+FINISH = 16 * MIB
 bf16 = jnp.bfloat16
 f32 = jnp.float32
 
@@ -63,13 +67,10 @@
     index = jnp.arange(1, SIDE, dtype=jnp.int32)
     table = axis_table(index, where_z, length_z)
     part = jnp.arange(group, dtype=jnp.int32)
-    inverse = jnp.where(part[:, None, None] == owner[None, None, :], table[None], 0.0)
-    inverse = inverse.reshape(group * HALF, -1)
     forward = jnp.where(
         part[None, :, None] == owner[:, None, None], table.T[:, None, :], 0.0
     )
-    forward = forward.reshape(-1, group * HALF)
-    return inverse.astype(bf16), split(forward)
+    return split(forward.reshape(-1, group * HALF))
 
 
 def across(eye, block):
@@ -123,41 +124,23 @@
             copies.append(
                 pltpu.make_async_copy(ref.at[at], fine.at[k, at], fine_sem.at[k, g])
             )
-    for copy in copies:
+    for copy in copies[4 : 4 + pairs] + copies[:4]:
         copy.start()
-    for copy in copies[:4]:
-        copy.wait()
 
     def send(k, first, count):
         part = (slice(None), pl.ds(first, count))
         return pltpu.make_async_copy(ready.at[part], out_ref.at[part], out_sem.at[k])
 
-    lane = lax.broadcasted_iota(jnp.int32, (1, LANES), 1)
-    line = jnp.zeros((1, LANES), f32)
-    for m in range(owned):
-        line = jnp.where(lane == owned + m, index[0, m].astype(f32), line)
-        line = jnp.where(lane == 2 * owned + m, index[1, m].astype(f32), line)
-    eye = identity(LANES)
-    for k in range(2):
-        padded = jnp.concatenate(
-            [lows[k].astype(f32), jnp.zeros((LANES - owned, levels), f32)], axis=0
-        ).astype(bf16)
-        for y in range(0, levels, LANES):
-            low[pl.ds(y, LANES), :] = across(eye, padded[:, y : y + LANES])
-        for y in range(rows):
-            tile[pl.ds(k * rows + y, devices, stride=groups), :] = (
-                low[pl.ds(y, devices, stride=rows), :] + line
-            )
-    ready[:, 2 * step :, :] = tile[...].astype(bf16).reshape(devices, groups, LANES)
-    sends = [send(2, 2 * step, groups)]
-    sends[0].start()
-    eye = identity(side)
+    sends = []
     for k in range(2):
         for g in range(pairs):
             copies[4 + k * pairs + g].wait()
+            if k + g == 0:
+                for copy in copies[4 + pairs :]:
+                    copy.start()
             block = fine[k, 2 * g : 2 * g + 2].reshape(side, levels)
             for y in range(0, levels, side):
-                turned = across(eye, block[:, y : y + side])
+                turned = block[:, y : y + side].astype(f32).T
                 at = y * groups + 2 * g
                 tall[pl.ds(at, side, stride=groups), :] = turned[:, :LANES]
                 tall[pl.ds(at + 1, side, stride=groups), :] = turned[:, LANES:]
@@ -166,25 +149,38 @@
         )
         sends.append(send(k, k * step, step))
         sends[-1].start()
+        if k == 1:
+            continue
+        for copy in copies[:4]:
+            copy.wait()
+        lane = lax.broadcasted_iota(jnp.int32, (1, LANES), 1)
+        line = jnp.zeros((1, LANES), f32)
+        for m in range(owned):
+            line = jnp.where(lane == owned + m, index[0, m].astype(f32), line)
+            line = jnp.where(lane == 2 * owned + m, index[1, m].astype(f32), line)
+        small = identity(LANES)
+        for h in range(2):
+            padded = jnp.concatenate(
+                [lows[h].astype(f32), jnp.zeros((LANES - owned, levels), f32)], axis=0
+            ).astype(bf16)
+            for y in range(0, levels, LANES):
+                low[pl.ds(y, LANES), :] = across(small, padded[:, y : y + LANES])
+            for y in range(rows):
+                tile[pl.ds(h * rows + y, devices, stride=groups), :] = (
+                    low[pl.ds(y, devices, stride=rows), :] + line
+                )
+        ready[:, 2 * step :, :] = tile[...].astype(bf16).reshape(devices, groups, LANES)
+        sends.append(send(2, 2 * step, groups))
+        sends[-1].start()
     for copy in sends:
         copy.wait()
 
 
 def middle_kernel(
     unitary,
-    got_hbm,
-    back_x_hbm,
-    x_hbm,
-    top_hbm,
-    z_top_hbm,
-    z_rest_hbm,
-    out_hbm,
     got_ref,
-    back_x_ref,
+    tables,
     x_ref,
-    top_ref,
-    z_top_ref,
-    z_rest_ref,
     out_ref,
     modes,
     left,
@@ -198,8 +194,6 @@
     cross,
     coefficients,
     picked,
-    in_sem,
-    out_sem,
 ):
     groups_x, groups_z, _, _ = got_ref.shape
     groups = 8
@@ -214,26 +208,7 @@
     low_half = lane < HALF
     which = lane // (LANES // 4)
 
-    everything = (slice(None), slice(None))
-    tiles = everything + (pl.ds(2 * step, groups),)
-    lines = everything + (pl.ds(0, 2 * step),)
-    fetches = [
-        pltpu.make_async_copy(source, target, in_sem.at[k])
-        for k, (source, target) in enumerate(
-            (
-                (got_hbm.at[tiles], got_ref.at[tiles]),
-                (back_x_hbm, back_x_ref),
-                (top_hbm, top_ref),
-                (got_hbm.at[lines], got_ref.at[lines]),
-                (x_hbm, x_ref),
-                (z_top_hbm, z_top_ref),
-                (z_rest_hbm, z_rest_ref),
-            )
-        )
-    ]
-    for fetch in fetches:
-        fetch.start()
-    fetches[0].wait()
+    width = groups_z * LANES
     modes[...] = got_ref[:, :, 2 * step :, :].astype(f32).reshape(devices * groups, LANES)
     first = modes[pl.ds(0, devices, stride=groups), :]
     turned = [first.T]
@@ -257,11 +232,11 @@
         right[at, :LANES] = jnp.where(wanted == index_z, 1.0, 0.0).astype(bf16)
         right[at, LANES:] = jnp.where(index_z == 0.0, 1.0, 0.0).astype(bf16)
     spectrum[...] = dot(left[...], right[...]).astype(bf16)
-    fetches[1].wait()
 
     def spread(k, parts):
         both = jnp.concatenate(parts, axis=1)
-        full = dot(back_x_ref[...], jnp.concatenate([both, both], axis=0))
+        back = tables[2 * width :, : 2 * PADDED]
+        full = dot(back, jnp.concatenate([both, both], axis=0))
         for y in range(len(parts)):
             part = [
                 full[p * points : (p + 1) * points, y * side : (y + 1) * side]
@@ -290,8 +265,6 @@
         )
     wave_top[...] = wave[...].reshape(2 * half_rows, side).astype(bf16)
     sums[...] = jnp.zeros_like(sums)
-    fetches[2].wait()
-    fetches[3].wait()
 
     def fine(j, k):
         parts = [
@@ -302,7 +275,7 @@
 
     def multiply(j, _):
         at = pl.ds(pl.multiple_of(j * side, side), side)
-        coarse = dot(wave_top[...], top_ref[:, at])
+        coarse = across(wave_top[...], tables[at, :])
         flat = mean[...].reshape(2 * half_rows, LANES)
         coarse = coarse + jnp.concatenate([flat, flat], axis=1)
         coarse_u, coarse_v = coarse[:half_rows], coarse[half_rows:]
@@ -320,10 +293,9 @@
             )
         return 0
 
-    lax.fori_loop(0, groups_z // 2, multiply, 0, unroll=UNROLL)
-    for fetch in fetches[4:]:
-        fetch.wait()
-    both = dot(products[...], z_top_ref[...]) + dot(products[...], z_rest_ref[...])
+    lax.fori_loop(0, groups_z // 2, multiply, 0, unroll=1)
+    both = dot(products[...], tables[:width, :])
+    both = both + dot(products[...], tables[width : 2 * width, :])
     coefficients[...] = both.reshape(2, groups_x, rows, groups, side)
 
     def project(k):
@@ -346,8 +318,9 @@
                 )
             stacks.append(jnp.concatenate(stack, axis=0))
         top, rest = halves(jnp.concatenate(stacks, axis=1))
-        outer = dot(x_ref[...], top)
-        outer = outer[:PADDED] + outer[PADDED:] + dot(x_ref[:PADDED], rest)
+        table_x = x_ref[...]
+        outer = dot(table_x, top)
+        outer = outer[:PADDED] + outer[PADDED:] + dot(table_x[:PADDED], rest)
         done = []
         for y in range(rows):
             waves = outer[:, y * side : y * side + LANES] * unitary
@@ -367,14 +340,28 @@
     spread(0, parts)
     wave_top[:half_rows] = wave[0].reshape(half_rows, side).astype(bf16)
 
-    kept = 72
+    def subtract(j, _):
+        at = pl.ds(pl.multiple_of(j * side, side), side)
+        restored = across(wave_top[:half_rows], tables[at, :])
+        flat = mean[0].reshape(half_rows, LANES)
+        restored = restored + jnp.concatenate([flat, flat], axis=1)
+        high = (cross[:, at] - unitary * restored).astype(bf16)
+        for e in range(2):
+            out_ref[:, 2 * j + e, :step, :] = high[:, e * LANES : (e + 1) * LANES].reshape(
+                groups_x, step, LANES
+            )
+        return 0
+
+    lax.fori_loop(0, groups_z // 2, subtract, 0, unroll=1)
+
+    lines = 72
     parts = []
     for waves, constant in project(0):
         force = jnp.where(low_half, waves, jnp.where(lane == HALF, constant, 0.0))
         force = jnp.concatenate([force, jnp.zeros((LANES - PADDED, LANES), f32)], axis=0)
-        parts.append(force.T[:kept])
+        parts.append(force.T[:lines])
     force = jnp.concatenate(parts, axis=0).astype(bf16)[:, :PADDED]
-    line = lax.broadcasted_iota(jnp.int32, (kept, devices), 0)
+    line = lax.broadcasted_iota(jnp.int32, (lines, devices), 0)
     line = jnp.where(line < HALF, line + 1, jnp.where(line == HALF, 0, -1)).astype(f32)
     picked[...] = jnp.zeros_like(picked)
     for m in range(0, owned, 2):
@@ -382,7 +369,7 @@
         for e in range(2):
             hit = line == turned[0][2 * owned + m + e : 2 * owned + m + e + 1, :]
             for y in range(rows):
-                value = chosen[y * kept : (y + 1) * kept, e * devices : (e + 1) * devices]
+                value = chosen[y * lines : (y + 1) * lines, e * devices : (e + 1) * devices]
                 picked[y, m + e : m + e + 1, :] = jnp.sum(
                     jnp.where(hit, value, 0.0), axis=0, keepdims=True
                 )
@@ -392,84 +379,24 @@
     out_ref[:, :, step:, :] = (
         modes[...].astype(bf16).reshape(groups_x, groups_z, groups, LANES)
     )
-    part = everything + (pl.ds(step, groups),)
-    send_tiles = pltpu.make_async_copy(
-        out_ref.at[part], out_hbm.at[part], out_sem.at[groups_z // 2]
-    )
-    send_tiles.start()
-
-    def send(j):
-        part = (slice(None), pl.ds(2 * j, 2), pl.ds(0, step))
-        return pltpu.make_async_copy(out_ref.at[part], out_hbm.at[part], out_sem.at[j])
-
-    def subtract(j, _):
-        at = pl.ds(pl.multiple_of(j * side, side), side)
-        restored = dot(wave_top[:half_rows], top_ref[:, at])
-        flat = mean[0].reshape(half_rows, LANES)
-        restored = restored + jnp.concatenate([flat, flat], axis=1)
-        high = (cross[:, at] - unitary * restored).astype(bf16)
-        for e in range(2):
-            out_ref[:, 2 * j + e, :step, :] = high[:, e * LANES : (e + 1) * LANES].reshape(
-                groups_x, step, LANES
-            )
-        send(j).start()
-        return 0
-
-    lax.fori_loop(0, groups_z // 2, subtract, 0, unroll=UNROLL)
-    send_tiles.wait()
-
-    def drain(j, _):
-        send(j).wait()
-        return 0
-
-    lax.fori_loop(0, groups_z // 2, drain, 0)
-
-
-def finish_kernel(
-    got_hbm,
-    tau_hbm,
-    high_hbm,
-    low_ref,
-    got_ref,
-    tau_ref,
-    tall,
-    tile,
-    force,
-    ready,
-    got_sem,
-    tau_sem,
-    out_sem,
-):
-    devices = got_hbm.shape[0]
-    owned, levels, _ = tau_hbm.shape
+
+
+def finish_kernel(got_ref, tau_ref, high_hbm, low_ref, tall, tile, force, ready, out_sem):
+    devices = got_ref.shape[0]
+    owned, levels, _ = tau_ref.shape
     rows = levels // devices
     groups = high_hbm.shape[0]
     step = rows * groups
     chunk = LANES // rows
-    count = devices // chunk
-    fetches = []
-    for q in range(count):
-        at = pl.ds(q * chunk, chunk)
-        fetches.append(
-            pltpu.make_async_copy(got_hbm.at[at], got_ref.at[at], got_sem.at[q])
-        )
-    for m in range(owned):
-        fetches.append(
-            pltpu.make_async_copy(tau_hbm.at[m], tau_ref.at[m], tau_sem.at[m])
-        )
-    for fetch in fetches:
-        fetch.start()
-    eye = identity(LANES)
     sends = []
-    for q in range(count):
-        fetches[q].wait()
+    for q in range(devices // chunk):
         at = slice(q * chunk, (q + 1) * chunk)
         tall[...] = got_ref[at, :step, :].astype(f32).reshape(chunk * step, LANES)
-        where = pl.ds(q * LANES, LANES)
+        where = slice(q * LANES, (q + 1) * LANES)
         for g in range(groups):
-            column = tall[pl.ds(g, LANES, stride=groups), :].astype(bf16)
-            ready[g, :, q * LANES : (q + 1) * LANES] = across(eye, column).astype(bf16)
-        part = (slice(None), slice(None), where)
+            column = tall[pl.ds(g, LANES, stride=groups), :]
+            ready[g, :, where] = column.T.astype(bf16)
+        part = (slice(None), slice(None), pl.ds(q * LANES, LANES))
         sends.append(
             pltpu.make_async_copy(ready.at[part], high_hbm.at[part], out_sem.at[q])
         )
@@ -480,13 +407,24 @@
             pl.ds(y, devices, stride=groups), :
         ]
     vector = force[...].astype(bf16)
-    lane = lax.broadcasted_iota(jnp.int32, (levels, LANES), 1)
+    lane = lax.broadcasted_iota(jnp.int32, (1, LANES), 1)
     answer = jnp.zeros((levels, LANES), f32)
     for m in range(owned):
-        fetches[count + m].wait()
         answer = jnp.where(lane == m, dot(tau_ref[m], vector), answer)
     low_ref[...] = answer.T[:owned]
     for copy in sends:
+        copy.wait()
+
+
+def stage_kernel(*refs):
+    count = (len(refs) - 1) // 2
+    copies = [
+        pltpu.make_async_copy(refs[k], refs[count + k], refs[-1].at[k])
+        for k in range(count)
+    ]
+    for copy in copies:
+        copy.start()
+    for copy in copies:
         copy.wait()
 
 
@@ -509,6 +447,7 @@
     unitary = 1.0 / math.sqrt(length_x * length_z)
 
     anywhere = pl.BlockSpec(memory_space=pltpu.HBM)
+    near = pl.BlockSpec(memory_space=pltpu.VMEM)
     sent = pl.pallas_call(
         prepare_kernel,
         out_shape=jax.ShapeDtypeStruct((devices, 2 * step + groups, LANES), bf16),
@@ -527,7 +466,7 @@
             pltpu.SemaphoreType.DMA((2,)),
             pltpu.SemaphoreType.DMA((3,)),
         ],
-        compiler_params=pltpu.CompilerParams(vmem_limit_bytes=WHOLE),
+        compiler_params=pltpu.CompilerParams(vmem_limit_bytes=PREPARE),
         interpret=INTERPRET,
         name="prepare",
     )(
@@ -541,20 +480,28 @@
     got = lax.all_to_all(sent, AXES, 0, 0, tiled=True)
 
     forward_x, back_x = x_tables(groups_x, groups, group, length_x)
-    top, forward_z = z_tables(group, cells_z, length_z)
+    back_x = jnp.pad(back_x, ((0, 0), (0, side - 2 * PADDED)))
+    tables = jnp.concatenate([*z_tables(group, cells_z, length_z), back_x], axis=0)
+    kept = (tau_inverse, forward_x)
+    tau_inverse, staged_x = pl.pallas_call(
+        stage_kernel,
+        out_shape=[jax.ShapeDtypeStruct(a.shape, a.dtype) for a in kept],
+        in_specs=[anywhere] * len(kept),
+        out_specs=[near] * len(kept),
+        scratch_shapes=[pltpu.SemaphoreType.DMA((len(kept),))],
+        compiler_params=pltpu.CompilerParams(vmem_limit_bytes=STAGE),
+        cost_estimate=pl.CostEstimate(
+            flops=2**30, bytes_accessed=2**24, transcendentals=0
+        ),
+        interpret=INTERPRET,
+        name="stage",
+    )(*kept)
     sent = pl.pallas_call(
         functools.partial(middle_kernel, unitary),
         out_shape=jax.ShapeDtypeStruct((groups_x, groups_z, step + groups, LANES), bf16),
-        in_specs=[anywhere] * 6,
-        out_specs=anywhere,
+        in_specs=[near] * 3,
+        out_specs=near,
         scratch_shapes=[
-            pltpu.VMEM((groups_x, groups_z, 2 * step + groups, LANES), bf16),
-            pltpu.VMEM(back_x.shape, bf16),
-            pltpu.VMEM(forward_x.shape, bf16),
-            pltpu.VMEM(top.shape, bf16),
-            pltpu.VMEM(forward_z[0].shape, bf16),
-            pltpu.VMEM(forward_z[1].shape, bf16),
-            pltpu.VMEM((groups_x, groups_z, step + groups, LANES), bf16),
             pltpu.VMEM((devices * groups, LANES), f32),
             pltpu.VMEM(((2 * rows + 1) * PADDED, owned * devices), bf16),
             pltpu.VMEM((owned * devices, side), bf16),
@@ -567,18 +514,14 @@
             pltpu.VMEM((half_rows, width), f32),
             pltpu.VMEM((2, groups_x, rows, groups, side), f32),
             pltpu.VMEM((rows, LANES, devices), f32),
-            pltpu.SemaphoreType.DMA((7,)),
-            pltpu.SemaphoreType.DMA((groups_z // 2 + 1,)),
         ],
-        compiler_params=pltpu.CompilerParams(vmem_limit_bytes=WHOLE),
+        compiler_params=pltpu.CompilerParams(vmem_limit_bytes=MIDDLE),
         interpret=INTERPRET,
         name="middle",
     )(
         got.reshape(groups_x, groups_z, 2 * step + groups, LANES),
-        back_x,
-        forward_x,
-        top,
-        *forward_z,
+        tables,
+        staged_x,
     )
     got = lax.all_to_all(
         sent.reshape(devices, step + groups, LANES), AXES, 0, 0, tiled=True
@@ -590,20 +533,16 @@
             jax.ShapeDtypeStruct((groups, LANES, levels), bf16),
             jax.ShapeDtypeStruct((owned, levels), f32),
         ),
-        in_specs=[anywhere] * 2,
-        out_specs=(anywhere, pl.BlockSpec(memory_space=pltpu.VMEM)),
+        in_specs=[near] * 2,
+        out_specs=(anywhere, near),
         scratch_shapes=[
-            pltpu.VMEM((devices, step + groups, LANES), bf16),
-            pltpu.VMEM((owned, levels, levels), bf16),
             pltpu.VMEM((LANES * groups, LANES), f32),
             pltpu.VMEM((devices * groups, LANES), f32),
             pltpu.VMEM((levels, LANES), f32),
             pltpu.VMEM((groups, LANES, levels), bf16),
             pltpu.SemaphoreType.DMA((devices * rows // LANES,)),
-            pltpu.SemaphoreType.DMA((owned,)),
-            pltpu.SemaphoreType.DMA((devices * rows // LANES,)),
         ],
-        compiler_params=pltpu.CompilerParams(vmem_limit_bytes=WHOLE),
+        compiler_params=pltpu.CompilerParams(vmem_limit_bytes=FINISH),
         interpret=INTERPRET,
         name="finish",
     )(got, tau_inverse)

time: 104 us -> 92.1 us (0.89)
  Pallas kernels: 29.8 us -> 19 us
  local copies, waits for them, and re-layouts: 1.97 us -> 11.2 us
  waiting for transfers between devices: 20.8 us -> 16.2 us
  other arithmetic: 10.2 us -> 6.84 us
  blocking collectives: 27.8 us -> 26.3 us
    unnamed x2 -> x10, local copies, waits for them, and re-layouts: 0.01 us -> 8.23 us
    pallas_call x1, Pallas kernels: 11.8 us -> 3.99 us  [on_device(): pl.pallas_call(finish_kernel, out_shape=(jax.ShapeDtypeStruct((groups, LA...]
    all_to_all x1, waiting for transfers between devices: 20.8 us -> 16.2 us  [on_device(): got = lax.all_to_all(sent, AXES, 0, 0, tiled=True)]
    select_n x2 -> x1, other arithmetic: 4.58 us -> 2.14 us  [axis_table(): return jnp.where((index <= KL)[:, None], jnp.cos(angles), jnp.sin(angles))]
    pallas_call x1, Pallas kernels: 12.7 us -> 10.4 us  [on_device(): pl.pallas_call(functools.partial(middle_kernel, unitary), out_shape=jax.S...]
    concatenate x0 -> x1, other arithmetic: none -> 1.54 us  [on_device(): jnp.concatenate([*z_tables(group, cells_z, length_z), back_x], axis=0)]
    all_to_all x1, blocking collectives: 27.8 us -> 26.3 us  [on_device(): lax.all_to_all(sent.reshape(devices, step + groups, LANES), AXES, 0, 0, t...]
    pallas_call x1, Pallas kernels: 5.28 us -> 3.9 us  [on_device(): pl.pallas_call(prepare_kernel, out_shape=jax.ShapeDtypeStruct((devices, 2...]
  transfers between devices with their start and end apart: 1 -> 1, of which waited for: 1 -> 1; matrix products, arithmetic and copies ran while one was open for 12% -> 11% of each run, Pallas kernels for 0% -> 1%
where the time goes in v3:
time: 92.1 us; the launch traced here: 91.8 us
  blocking collectives  26.3 us (29%)
  Pallas kernels  19 us (21%)
  waiting for transfers between devices  16.2 us (18%)
  starting transfers between devices  11.5 us (12%)
  local copies, waits for them, and re-layouts  11.2 us (12%)
  other arithmetic  6.84 us (7%)
    all_to_all x1, blocking collectives, on_device(): lax.all_to_all(sent.reshape(devices, step + groups, LANES), AXES, 0, 0, t...  26.3 us
    all_to_all x1, waiting for transfers between devices, on_device(): got = lax.all_to_all(sent, AXES, 0, 0, tiled=True)  16.2 us
    all_to_all x1, starting transfers between devices, on_device(): got = lax.all_to_all(sent, AXES, 0, 0, tiled=True)  11.5 us
    pallas_call x1, Pallas kernels, on_device(): pl.pallas_call(functools.partial(middle_kernel, unitary), out_shape=jax.S...  10.4 us
    unnamed x10, local copies, waits for them, and re-layouts  8.23 us
    pallas_call x1, Pallas kernels, on_device(): pl.pallas_call(finish_kernel, out_shape=(jax.ShapeDtypeStruct((groups, LA...  3.99 us
    pallas_call x1, Pallas kernels, on_device(): pl.pallas_call(prepare_kernel, out_shape=jax.ShapeDtypeStruct((devices, 2...  3.9 us
    select_n x1, local copies, waits for them, and re-layouts, z_tables(): jnp.where(part[None, :, None] == owner[:, None, None], table.T[:, None, :...  2.91 us
  transfers between devices with their start and end apart: 1, of which 1 were waited for; matrix products, arithmetic and copies ran while one was open for 11% of the time, Pallas kernels for 1%

profile of v3, /device:TPU:1, one launch (start us, length us, event | category | flops | bytes accessed | tf_op | source)
XLA Modules:
  0.0 91.8 jit_solution(3747194437308347930)
XLA Ops:
  0.6 3.9 %prepare.1 = bf16[128,72,128]{2,1,0:T(8,128)(2,1)} custom-call(bf16[8,128,512]{2,1,0:T(8,128)(2,1)} %bitcast.9, bf16[8,128,512]{2,1,0:T(8,128)(2,1)} %bitcast.10, bf16[16,512]{1,0:T(8,128)(2,1)} %low_u_ref.1, bf16[16,512]{1,0:T(8,128)(2,1)} %low_v_ref.1, s32[16]{0:T(128)} %kx_ref.1, s32[16]{0:T(128)} %kz_ref.1), custom_call_target="tpu_custom_call" | custom-call | tf_op jit(solution)/shard_map/prepare/pallas_call | solution.py:451
  4.5 11.5 %all-to-all-start = ((bf16[128,72,128]{2,1,0:T(8,128)(2,1)}), bf16[128,72,128]{2,1,0:T(8,128)(2,1)S(1)}, u32[]{:S(2)}, u32[]{:S(2)}) async-start(bf16[128,72,128]{2,1,0:T(8,128)(2,1)} %prepare.1), calls=%async_computation | async-start | bytes 4718592 | tf_op jit(solution)/shard_map/all_to_all | solution.py:480
  16.1 0.1 broadcast_add_fusion
  16.2 2.1 %sine_select_fusion = f32[2048,64]{0,1:T(8,128)S(1)} fusion(s32[2048]{0:T(1024)S(1)} %fusion.24, s32[64]{0:T(128)S(1)} %add_select_fusion.7, pred[64]{0:T(512)(128)(4,1)S(1)} %fusion.27), kind=kLoop, calls=%fused_computation.13 | loop fusion | flops 1966080 | bytes 532800 | tf_op jit(solution)/shard_map/jit(_where)/select_n | solution.py:32
  18.3 1.6 %broadcast_select_fusion = f32[2048,4,64]{0,2,1:T(8,128)} fusion(f32[2048,64]{0,1:T(8,128)S(1)} %sine_select_fusion, pred[2048,4]{0,1:T(4,128)(4,1)S(1)} %iota_compare_fusion.1), kind=kLoop, calls=%fused_computation.4 | loop fusion | flops 524288 | bytes 2629632 | tf_op jit(solution)/shard_map/jit(_where)/select_n | solution.py:70
  19.9 0.1 add.188
  20.0 2.9 %copy.9 = f32[2048,256]{1,0:T(8,128)} copy(f32[2048,256]{0,1:T(8,128)} %bitcast.8) | data formatting | bytes 4194304 | tf_op jit(solution)/shard_map/jit(_where)/select_n | solution.py:70
  22.9 0.4 reduce-precision_convert_fusion.2
  23.4 0.0 copy-start.3
  23.4 3.4 %copy-done.3 = bf16[16,512,512]{2,1,0:T(8,128)(2,1)S(1)} copy-done((bf16[16,512,512]{2,1,0:T(8,128)(2,1)S(1)}, bf16[16,512,512]{2,1,0:T(8,128)(2,1)}, u32[]{:S(2)}) %copy-start.3) | copy-done | bytes 8388632
  26.7 0.0 copy-start.4
  26.7 0.7 stage.1
  27.4 0.0 copy-start.1
  27.4 3.2 %copy-done.1 = bf16[16,512,512]{2,1,0:T(8,128)(2,1)} copy-done((bf16[16,512,512]{2,1,0:T(8,128)(2,1)}, bf16[16,512,512]{2,1,0:T(8,128)(2,1)S(1)}, u32[]{:S(2)}) %copy-start.1) | copy-done | bytes 8388632
  30.7 0.6 reduce-precision_convert_fusion.1
  31.3 0.1 fusion.10
  31.4 0.0 copy-done.4
  31.4 0.3 reduce-precision_convert_fusion
  31.7 1.5 %pad_maximum_fusion.tables = bf16[4352,256]{1,0:T(8,128)(2,1)} fusion(bf16[256,256]{1,0:T(8,128)(2,1)S(1)} %fusion.10, bf16[2048,256]{1,0:T(8,128)(2,1)S(1)} %get-tuple-element.11, bf16[2048,256]{1,0:T(8,128)(2,1)S(1)} %get-tuple-element.10), kind=kLoop, calls=%fused_computation.2 | loop fusion | flops 6684672 | bytes 4456448 | tf_op jit(solution)/shard_map/concatenate | solution.py:484
  33.3 16.2 %all-to-all-done = bf16[128,72,128]{2,1,0:T(8,128)(2,1)S(1)} async-done(((bf16[128,72,128]{2,1,0:T(8,128)(2,1)}), bf16[128,72,128]{2,1,0:T(8,128)(2,1)S(1)}, u32[]{:S(2)}, u32[]{:S(2)}) %all-to-all-start) | async-done | bytes 2359328 | tf_op jit(solution)/shard_map/all_to_all | solution.py:480
  49.5 0.0 copy-start
  49.5 1.6 %copy-done = bf16[4352,256]{1,0:T(8,128)(2,1)S(1)} copy-done((bf16[4352,256]{1,0:T(8,128)(2,1)S(1)}, bf16[4352,256]{1,0:T(8,128)(2,1)}, u32[]{:S(2)}) %copy-start) | copy-done | bytes 2228248
  51.1 0.0 copy-start.2
  51.1 10.4 %middle.1 = bf16[8,16,40,128]{3,2,1,0:T(8,128)(2,1)S(1)} custom-call(bf16[8,16,72,128]{3,2,1,0:T(8,128)(2,1)S(1)} %bitcast.6, bf16[4352,256]{1,0:T(8,128)(2,1)S(1)} %copy-done, bf16[160,256]{1,0:T(8,128)(2,1)S(1)} %get-tuple-element.6.x_ref), custom_call_target="tpu_custom_call" | custom-call | tf_op jit(solution)/shard_map/middle/pallas_call | solution.py:499
  61.6 26.3 %all_to_all.10.got_ref = bf16[128,40,128]{2,1,0:T(8,128)(2,1)S(1)} all-to-all(bf16[128,40,128]{2,1,0:T(8,128)(2,1)S(1)} %bitcast.7), channel_id=1, replica_groups=mesh['gx'=8,'gz'=16] {'gx','gz'}, dimensions={0} | all-to-all | bytes 2621440 | tf_op jit(solution)/shard_map/all_to_all | solution.py:526
  87.8 0.0 copy-done.2
  87.8 4.0 %finish.1 = (bf16[8,128,512]{2,1,0:T(8,128)(2,1)}, f32[16,512]{1,0:T(8,128)}) custom-call(bf16[128,40,128]{2,1,0:T(8,128)(2,1)S(1)} %all_to_all.10.got_ref, bf16[16,512,512]{2,1,0:T(8,128)(2,1)S(1)} %copy-done.2), custom_call_target="tpu_custom_call" | custom-call | tf_op jit(solution)/shard_map/finish/pallas_call | solution.py:530
  (10 shorter events, 0.1 us)
Async XLA Ops:
  4.5 44.9 %all-to-all-start = ((bf16[128,72,128]{2,1,0:T(8,128)(2,1)}), bf16[128,72,128]{2,1,0:T(8,128)(2,1)S(1)}, u32[]{:S(2)}, u32[]{:S(2)}) async-start(bf16[128,72,128]{2,1,0:T(8,128)(2,1)} %prepare.1), calls=%async_computation | async-start | bytes 4718592 | tf_op jit(solution)/shard_map/all_to_all | solution.py:480
  23.4 3.4 %copy-start.3 = (bf16[16,512,512]{2,1,0:T(8,128)(2,1)S(1)}, bf16[16,512,512]{2,1,0:T(8,128)(2,1)}, u32[]{:S(2)}) copy-start(bf16[16,512,512]{2,1,0:T(8,128)(2,1)} %refs_0_.1) | copy-start | bytes 25165828
  26.7 4.7 %copy-start.4 = (f32[2048,256]{1,0:T(8,128)S(1)}, f32[2048,256]{1,0:T(8,128)}, u32[]{:S(2)}) copy-start(f32[2048,256]{1,0:T(8,128)} %copy.9) | copy-start | bytes 6291460
  27.4 3.2 %copy-start.1 = (bf16[16,512,512]{2,1,0:T(8,128)(2,1)}, bf16[16,512,512]{2,1,0:T(8,128)(2,1)S(1)}, u32[]{:S(2)}) copy-start(bf16[16,512,512]{2,1,0:T(8,128)(2,1)S(1)} %get-tuple-element.7.tau_ref) | copy-start | bytes 25165828
  49.5 1.6 %copy-start = (bf16[4352,256]{1,0:T(8,128)(2,1)S(1)}, bf16[4352,256]{1,0:T(8,128)(2,1)}, u32[]{:S(2)}) copy-start(bf16[4352,256]{1,0:T(8,128)(2,1)} %pad_maximum_fusion.tables) | copy-start | bytes 6684676
  51.1 36.7 %copy-start.2 = (bf16[16,512,512]{2,1,0:T(8,128)(2,1)S(1)}, bf16[16,512,512]{2,1,0:T(8,128)(2,1)}, u32[]{:S(2)}) copy-start(bf16[16,512,512]{2,1,0:T(8,128)(2,1)} %copy-done.1) | copy-start | bytes 25165828

commit v4 on v3

--- a/solution.py
+++ b/solution.py
@@ -60,17 +60,11 @@
     return forward, jnp.concatenate([top, rest], axis=1)
 
 
-def z_tables(group, cells_z, length_z):
+def z_table(group, cells_z, length_z):
     column = jnp.arange(length_z * group, dtype=jnp.int32)
     where_z = column // (group * cells_z) * cells_z + column % cells_z
-    owner = column // cells_z % group
-    index = jnp.arange(1, SIDE, dtype=jnp.int32)
-    table = axis_table(index, where_z, length_z)
-    part = jnp.arange(group, dtype=jnp.int32)
-    forward = jnp.where(
-        part[None, :, None] == owner[:, None, None], table.T[:, None, :], 0.0
-    )
-    return split(forward.reshape(-1, group * HALF))
+    index = 1 + jnp.arange(LANES, dtype=jnp.int32) % HALF
+    return axis_table(index, where_z, length_z).T.astype(bf16)
 
 
 def across(eye, block):
@@ -179,9 +173,11 @@
 def middle_kernel(
     unitary,
     got_ref,
-    tables,
     x_ref,
+    back_x_ref,
+    base_ref,
     out_ref,
+    table,
     modes,
     left,
     right,
@@ -209,6 +205,13 @@
     which = lane // (LANES // 4)
 
     width = groups_z * LANES
+    owner = lax.broadcasted_iota(jnp.int32, (LANES, side), 0) // (LANES // 4)
+    part = lax.broadcasted_iota(jnp.int32, (LANES, side), 1) // HALF
+    own = jnp.where(owner == part, 1.0, 0.0).astype(bf16)
+    for j in range(groups_z):
+        at = slice(j * LANES, (j + 1) * LANES)
+        table[at, :] = jnp.concatenate([base_ref[at, :]] * 2, axis=1) * own
+
     modes[...] = got_ref[:, :, 2 * step :, :].astype(f32).reshape(devices * groups, LANES)
     first = modes[pl.ds(0, devices, stride=groups), :]
     turned = [first.T]
@@ -235,8 +238,7 @@
 
     def spread(k, parts):
         both = jnp.concatenate(parts, axis=1)
-        back = tables[2 * width :, : 2 * PADDED]
-        full = dot(back, jnp.concatenate([both, both], axis=0))
+        full = dot(back_x_ref[...], jnp.concatenate([both, both], axis=0))
         for y in range(len(parts)):
             part = [
                 full[p * points : (p + 1) * points, y * side : (y + 1) * side]
@@ -275,7 +277,7 @@
 
     def multiply(j, _):
         at = pl.ds(pl.multiple_of(j * side, side), side)
-        coarse = across(wave_top[...], tables[at, :])
+        coarse = across(wave_top[...], table[at, :])
         flat = mean[...].reshape(2 * half_rows, LANES)
         coarse = coarse + jnp.concatenate([flat, flat], axis=1)
         coarse_u, coarse_v = coarse[:half_rows], coarse[half_rows:]
@@ -294,8 +296,7 @@
         return 0
 
     lax.fori_loop(0, groups_z // 2, multiply, 0, unroll=1)
-    both = dot(products[...], tables[:width, :])
-    both = both + dot(products[...], tables[width : 2 * width, :])
+    both = dot(products[...], table[...])
     coefficients[...] = both.reshape(2, groups_x, rows, groups, side)
 
     def project(k):
@@ -342,7 +343,7 @@
 
     def subtract(j, _):
         at = pl.ds(pl.multiple_of(j * side, side), side)
-        restored = across(wave_top[:half_rows], tables[at, :])
+        restored = across(wave_top[:half_rows], table[at, :])
         flat = mean[0].reshape(half_rows, LANES)
         restored = restored + jnp.concatenate([flat, flat], axis=1)
         high = (cross[:, at] - unitary * restored).astype(bf16)
@@ -409,8 +410,10 @@
     vector = force[...].astype(bf16)
     lane = lax.broadcasted_iota(jnp.int32, (1, LANES), 1)
     answer = jnp.zeros((levels, LANES), f32)
-    for m in range(owned):
-        answer = jnp.where(lane == m, dot(tau_ref[m], vector), answer)
+    for m in range(0, owned, 2):
+        pair = dot(tau_ref[m : m + 2].reshape(2 * levels, levels), vector)
+        answer = jnp.where(lane == m, pair[:levels], answer)
+        answer = jnp.where(lane == m + 1, pair[levels:], answer)
     low_ref[...] = answer.T[:owned]
     for copy in sends:
         copy.wait()
@@ -480,10 +483,8 @@
     got = lax.all_to_all(sent, AXES, 0, 0, tiled=True)
 
     forward_x, back_x = x_tables(groups_x, groups, group, length_x)
-    back_x = jnp.pad(back_x, ((0, 0), (0, side - 2 * PADDED)))
-    tables = jnp.concatenate([*z_tables(group, cells_z, length_z), back_x], axis=0)
-    kept = (tau_inverse, forward_x)
-    tau_inverse, staged_x = pl.pallas_call(
+    kept = (forward_x, back_x, z_table(group, cells_z, length_z))
+    tables = pl.pallas_call(
         stage_kernel,
         out_shape=[jax.ShapeDtypeStruct(a.shape, a.dtype) for a in kept],
         in_specs=[anywhere] * len(kept),
@@ -499,9 +500,10 @@
     sent = pl.pallas_call(
         functools.partial(middle_kernel, unitary),
         out_shape=jax.ShapeDtypeStruct((groups_x, groups_z, step + groups, LANES), bf16),
-        in_specs=[near] * 3,
+        in_specs=[near] * 4,
         out_specs=near,
         scratch_shapes=[
+            pltpu.VMEM((width, side), bf16),
             pltpu.VMEM((devices * groups, LANES), f32),
             pltpu.VMEM(((2 * rows + 1) * PADDED, owned * devices), bf16),
             pltpu.VMEM((owned * devices, side), bf16),
@@ -516,12 +518,14 @@
             pltpu.VMEM((rows, LANES, devices), f32),
         ],
         compiler_params=pltpu.CompilerParams(vmem_limit_bytes=MIDDLE),
+        cost_estimate=pl.CostEstimate(
+            flops=2**33, bytes_accessed=2**22, transcendentals=0
+        ),
         interpret=INTERPRET,
         name="middle",
     )(
         got.reshape(groups_x, groups_z, 2 * step + groups, LANES),
-        tables,
-        staged_x,
+        *tables,
     )
     got = lax.all_to_all(
         sent.reshape(devices, step + groups, LANES), AXES, 0, 0, tiled=True

time: 92.1 us -> 89.9 us (0.976)
  local copies, waits for them, and re-layouts: 11.2 us -> 0.1 us
  waiting for transfers between devices: 16.2 us -> 26.8 us
    all_to_all x1, waiting for transfers between devices: 16.2 us -> 26.8 us  [on_device(): got = lax.all_to_all(sent, AXES, 0, 0, tiled=True)]
    unnamed x10 -> x4, local copies, waits for them, and re-layouts: 8.23 us -> 0.01 us
    convert_element_type x0 -> x1, other arithmetic: none -> 4.82 us  [z_table(): return axis_table(index, where_z, length_z).T.astype(bf16)]
    select_n x3 -> x0, other arithmetic: 3.71 us -> none  [the longest x1 2.14 us: axis_table(): return jnp.where((index <= KL)[:, None], jnp.cos(angles), jnp.sin(angles))]
    select_n x1 -> x0, local copies, waits for them, and re-layouts: 2.91 us -> none  [z_tables(): jnp.where(part[None, :, None] == owner[:, None, None], table.T[:, None, :...]
    concatenate x1 -> x0, other arithmetic: 1.54 us -> none  [on_device(): jnp.concatenate([*z_tables(group, cells_z, length_z), back_x], axis=0)]
  transfers between devices with their start and end apart: 1 -> 1, of which waited for: 1 -> 1; matrix products, arithmetic and copies ran while one was open for 11% -> 7% of each run, Pallas kernels for 1% -> 0%
where the time goes in v4:
time: 89.9 us; the launch traced here: 89.7 us
  waiting for transfers between devices  26.8 us (30%)
  blocking collectives  26.2 us (29%)
  Pallas kernels  18.2 us (20%)
  starting transfers between devices  11.5 us (13%)
  other arithmetic  6.08 us (7%)
    all_to_all x1, waiting for transfers between devices, on_device(): got = lax.all_to_all(sent, AXES, 0, 0, tiled=True)  26.8 us
    all_to_all x1, blocking collectives, on_device(): lax.all_to_all(sent.reshape(devices, step + groups, LANES), AXES, 0, 0, t...  26.2 us
    all_to_all x1, starting transfers between devices, on_device(): got = lax.all_to_all(sent, AXES, 0, 0, tiled=True)  11.5 us
    pallas_call x1, Pallas kernels, on_device(): pl.pallas_call(functools.partial(middle_kernel, unitary), out_shape=jax.S...  9.96 us
    convert_element_type x1, other arithmetic, z_table(): return axis_table(index, where_z, length_z).T.astype(bf16)  4.82 us
    pallas_call x1, Pallas kernels, on_device(): pl.pallas_call(finish_kernel, out_shape=(jax.ShapeDtypeStruct((groups, LA...  3.97 us
    pallas_call x1, Pallas kernels, on_device(): pl.pallas_call(prepare_kernel, out_shape=jax.ShapeDtypeStruct((devices, 2...  3.88 us
  transfers between devices with their start and end apart: 1, of which 1 were waited for; matrix products, arithmetic and copies ran while one was open for 7% of the time, Pallas kernels for 0%

profile of v4, /device:TPU:1, one launch (start us, length us, event | category | flops | bytes accessed | tf_op | source)
XLA Modules:
  0.0 89.7 jit_solution(13414969052476891067)
XLA Ops:
  0.6 3.9 %prepare.1 = bf16[128,72,128]{2,1,0:T(8,128)(2,1)} custom-call(bf16[8,128,512]{2,1,0:T(8,128)(2,1)} %bitcast.9, bf16[8,128,512]{2,1,0:T(8,128)(2,1)} %bitcast.10, bf16[16,512]{1,0:T(8,128)(2,1)} %low_u_ref.1, bf16[16,512]{1,0:T(8,128)(2,1)} %low_v_ref.1, s32[16]{0:T(128)} %kx_ref.1, s32[16]{0:T(128)} %kz_ref.1), custom_call_target="tpu_custom_call" | custom-call | tf_op jit(solution)/shard_map/prepare/pallas_call | solution.py:454
  4.5 11.5 %all-to-all-start = ((bf16[128,72,128]{2,1,0:T(8,128)(2,1)}), bf16[128,72,128]{2,1,0:T(8,128)(2,1)S(1)}, u32[]{:S(2)}, u32[]{:S(2)}) async-start(bf16[128,72,128]{2,1,0:T(8,128)(2,1)} %prepare.1), calls=%async_computation | async-start | bytes 4718592 | tf_op jit(solution)/shard_map/all_to_all | solution.py:483
  16.0 0.1 broadcast_add_fusion
  16.1 0.1 add.166
  16.3 0.4 reduce-precision_convert_fusion.1
  16.7 0.6 reduce-precision_convert_fusion
  17.3 0.1 pad_maximum_fusion.refs_1_
  17.4 4.8 %select_convert_fusion.refs_2_ = bf16[2048,128]{1,0:T(8,128)(2,1)S(1)} fusion(s32[2048]{0:T(1024)S(1)} %fusion.16, s32[128]{0:T(128)S(1)} %add_select_fusion.5, pred[128]{0:T(512)(128)(4,1)S(1)} %add_compare_fusion), kind=kLoop, calls=%fused_computation.8 | loop fusion | flops 4194304 | bytes 533120 | tf_op jit(solution)/shard_map/convert_element_type | solution.py:67
  22.3 0.3 stage.1
  22.6 26.8 %all-to-all-done = bf16[128,72,128]{2,1,0:T(8,128)(2,1)S(1)} async-done(((bf16[128,72,128]{2,1,0:T(8,128)(2,1)}), bf16[128,72,128]{2,1,0:T(8,128)(2,1)S(1)}, u32[]{:S(2)}, u32[]{:S(2)}) %all-to-all-start) | async-done | bytes 2359328 | tf_op jit(solution)/shard_map/all_to_all | solution.py:483
  49.5 0.0 slice-start
  49.5 0.0 slice-start.1
  49.5 10.0 %middle.1 = bf16[8,16,40,128]{3,2,1,0:T(8,128)(2,1)S(1)} custom-call(bf16[8,16,72,128]{3,2,1,0:T(8,128)(2,1)S(1)} %bitcast.7, bf16[160,256]{1,0:T(8,128)(2,1)S(1)} %get-tuple-element.7.x_ref, bf16[256,160]{1,0:T(8,128)(2,1)S(1)} %get-tuple-element.8.back_x_ref, bf16[2048,128]{1,0:T(8,128)(2,1)S(1)} %get-tuple-element.9.base_ref), custom_call_target="tpu_custom_call" | custom-call | flops 8589934592 | bytes 4194304 | tf_op jit(solution)/shard_map/middle/pallas_call | solution.py:500
  59.4 26.2 %all_to_all.10.got_ref = bf16[128,40,128]{2,1,0:T(8,128)(2,1)S(1)} all-to-all(bf16[128,40,128]{2,1,0:T(8,128)(2,1)S(1)} %bitcast.8), channel_id=1, replica_groups=mesh['gx'=8,'gz'=16] {'gx','gz'}, dimensions={0} | all-to-all | bytes 2621440 | tf_op jit(solution)/shard_map/all_to_all | solution.py:530
  85.7 0.0 slice-done
  85.7 0.0 slice-done.1
  85.7 4.0 %finish.1 = (bf16[8,128,512]{2,1,0:T(8,128)(2,1)}, f32[16,512]{1,0:T(8,128)}) custom-call(bf16[128,40,128]{2,1,0:T(8,128)(2,1)S(1)} %all_to_all.10.got_ref, bf16[16,512,512]{2,1,0:T(8,128)(2,1)S(1)} %bitcast.6), custom_call_target="tpu_custom_call" | custom-call | tf_op jit(solution)/shard_map/finish/pallas_call | solution.py:534
  (9 shorter events, 0.0 us)
Async XLA Ops:
  4.5 44.9 %all-to-all-start = ((bf16[128,72,128]{2,1,0:T(8,128)(2,1)}), bf16[128,72,128]{2,1,0:T(8,128)(2,1)S(1)}, u32[]{:S(2)}, u32[]{:S(2)}) async-start(bf16[128,72,128]{2,1,0:T(8,128)(2,1)} %prepare.1), calls=%async_computation | async-start | bytes 4718592 | tf_op jit(solution)/shard_map/all_to_all | solution.py:483
  49.5 36.2 %slice-start = ((s8[8388608]{0:T(1024)(128)(4,1)}), s8[4194304]{0:T(1024)(128)(4,1)S(1)}, s32[]{:S(2)}) async-start(s8[8388608]{0:T(1024)(128)(4,1)} %bitcast.5), calls=%async_computation.2 | async-start | bytes 8388608
  49.5 36.2 %slice-start.1 = ((s8[8388608]{0:T(1024)(128)(4,1)}), s8[4194304]{0:T(1024)(128)(4,1)S(1)}, s32[]{:S(2)}) async-start(s8[8388608]{0:T(1024)(128)(4,1)} %bitcast.5), calls=%async_computation.3 | async-start | bytes 8388608

commit v5 on v4

--- a/solution.py
+++ b/solution.py
@@ -295,7 +295,7 @@
             )
         return 0
 
-    lax.fori_loop(0, groups_z // 2, multiply, 0, unroll=1)
+    lax.fori_loop(0, groups_z // 2, multiply, 0, unroll=8)
     both = dot(products[...], table[...])
     coefficients[...] = both.reshape(2, groups_x, rows, groups, side)
 
@@ -353,7 +353,7 @@
             )
         return 0
 
-    lax.fori_loop(0, groups_z // 2, subtract, 0, unroll=1)
+    lax.fori_loop(0, groups_z // 2, subtract, 0, unroll=8)
 
     lines = 72
     parts = []

time: 89.9 us -> 86.9 us (0.967)
  Pallas kernels: 18.2 us -> 15.1 us
    pallas_call x1, Pallas kernels: 9.96 us -> 6.93 us  [on_device(): pl.pallas_call(functools.partial(middle_kernel, unitary), out_shape=jax.S...]
where the time goes in v5:
time: 86.9 us; the launch traced here: 86.6 us
  waiting for transfers between devices  26.8 us (31%)
  blocking collectives  26.2 us (30%)
  Pallas kernels  15.1 us (17%)
  starting transfers between devices  11.5 us (13%)
  other arithmetic  6.08 us (7%)
    all_to_all x1, waiting for transfers between devices, on_device(): got = lax.all_to_all(sent, AXES, 0, 0, tiled=True)  26.8 us
    all_to_all x1, blocking collectives, on_device(): lax.all_to_all(sent.reshape(devices, step + groups, LANES), AXES, 0, 0, t...  26.2 us
    all_to_all x1, starting transfers between devices, on_device(): got = lax.all_to_all(sent, AXES, 0, 0, tiled=True)  11.5 us
    pallas_call x1, Pallas kernels, on_device(): pl.pallas_call(functools.partial(middle_kernel, unitary), out_shape=jax.S...  6.93 us
    convert_element_type x1, other arithmetic, z_table(): return axis_table(index, where_z, length_z).T.astype(bf16)  4.82 us
    pallas_call x1, Pallas kernels, on_device(): pl.pallas_call(finish_kernel, out_shape=(jax.ShapeDtypeStruct((groups, LA...  3.97 us
    pallas_call x1, Pallas kernels, on_device(): pl.pallas_call(prepare_kernel, out_shape=jax.ShapeDtypeStruct((devices, 2...  3.88 us
  transfers between devices with their start and end apart: 1, of which 1 were waited for; matrix products, arithmetic and copies ran while one was open for 7% of the time, Pallas kernels for 0%

profile of v5, /device:TPU:1, one launch (start us, length us, event | category | flops | bytes accessed | tf_op | source)
XLA Modules:
  0.0 86.6 jit_solution(183828143513046166)
XLA Ops:
  0.6 3.9 %prepare.1 = bf16[128,72,128]{2,1,0:T(8,128)(2,1)} custom-call(bf16[8,128,512]{2,1,0:T(8,128)(2,1)} %bitcast.9, bf16[8,128,512]{2,1,0:T(8,128)(2,1)} %bitcast.10, bf16[16,512]{1,0:T(8,128)(2,1)} %low_u_ref.1, bf16[16,512]{1,0:T(8,128)(2,1)} %low_v_ref.1, s32[16]{0:T(128)} %kx_ref.1, s32[16]{0:T(128)} %kz_ref.1), custom_call_target="tpu_custom_call" | custom-call | tf_op jit(solution)/shard_map/prepare/pallas_call | solution.py:454
  4.5 11.5 %all-to-all-start = ((bf16[128,72,128]{2,1,0:T(8,128)(2,1)}), bf16[128,72,128]{2,1,0:T(8,128)(2,1)S(1)}, u32[]{:S(2)}, u32[]{:S(2)}) async-start(bf16[128,72,128]{2,1,0:T(8,128)(2,1)} %prepare.1), calls=%async_computation | async-start | bytes 4718592 | tf_op jit(solution)/shard_map/all_to_all | solution.py:483
  16.0 0.1 broadcast_add_fusion
  16.1 0.1 add.166
  16.3 0.4 reduce-precision_convert_fusion.1
  16.7 0.6 reduce-precision_convert_fusion
  17.3 0.1 pad_maximum_fusion.refs_1_
  17.4 4.8 %select_convert_fusion.refs_2_ = bf16[2048,128]{1,0:T(8,128)(2,1)S(1)} fusion(s32[2048]{0:T(1024)S(1)} %fusion.16, s32[128]{0:T(128)S(1)} %add_select_fusion.5, pred[128]{0:T(512)(128)(4,1)S(1)} %add_compare_fusion), kind=kLoop, calls=%fused_computation.8 | loop fusion | flops 4194304 | bytes 533120 | tf_op jit(solution)/shard_map/convert_element_type | solution.py:67
  22.3 0.3 stage.1
  22.6 26.8 %all-to-all-done = bf16[128,72,128]{2,1,0:T(8,128)(2,1)S(1)} async-done(((bf16[128,72,128]{2,1,0:T(8,128)(2,1)}), bf16[128,72,128]{2,1,0:T(8,128)(2,1)S(1)}, u32[]{:S(2)}, u32[]{:S(2)}) %all-to-all-start) | async-done | bytes 2359328 | tf_op jit(solution)/shard_map/all_to_all | solution.py:483
  49.5 0.0 slice-start
  49.5 0.0 slice-start.1
  49.5 6.9 %middle.1 = bf16[8,16,40,128]{3,2,1,0:T(8,128)(2,1)S(1)} custom-call(bf16[8,16,72,128]{3,2,1,0:T(8,128)(2,1)S(1)} %bitcast.7, bf16[160,256]{1,0:T(8,128)(2,1)S(1)} %get-tuple-element.7.x_ref, bf16[256,160]{1,0:T(8,128)(2,1)S(1)} %get-tuple-element.8.back_x_ref, bf16[2048,128]{1,0:T(8,128)(2,1)S(1)} %get-tuple-element.9.base_ref), custom_call_target="tpu_custom_call" | custom-call | flops 8589934592 | bytes 4194304 | tf_op jit(solution)/shard_map/middle/pallas_call | solution.py:500
  56.4 26.2 %all_to_all.10.got_ref = bf16[128,40,128]{2,1,0:T(8,128)(2,1)S(1)} all-to-all(bf16[128,40,128]{2,1,0:T(8,128)(2,1)S(1)} %bitcast.8), channel_id=1, replica_groups=mesh['gx'=8,'gz'=16] {'gx','gz'}, dimensions={0} | all-to-all | bytes 2621440 | tf_op jit(solution)/shard_map/all_to_all | solution.py:530
  82.7 0.0 slice-done
  82.7 0.0 slice-done.1
  82.7 4.0 %finish.1 = (bf16[8,128,512]{2,1,0:T(8,128)(2,1)}, f32[16,512]{1,0:T(8,128)}) custom-call(bf16[128,40,128]{2,1,0:T(8,128)(2,1)S(1)} %all_to_all.10.got_ref, bf16[16,512,512]{2,1,0:T(8,128)(2,1)S(1)} %bitcast.6), custom_call_target="tpu_custom_call" | custom-call | tf_op jit(solution)/shard_map/finish/pallas_call | solution.py:534
  (9 shorter events, 0.0 us)
Async XLA Ops:
  4.5 44.9 %all-to-all-start = ((bf16[128,72,128]{2,1,0:T(8,128)(2,1)}), bf16[128,72,128]{2,1,0:T(8,128)(2,1)S(1)}, u32[]{:S(2)}, u32[]{:S(2)}) async-start(bf16[128,72,128]{2,1,0:T(8,128)(2,1)} %prepare.1), calls=%async_computation | async-start | bytes 4718592 | tf_op jit(solution)/shard_map/all_to_all | solution.py:483
  49.5 33.2 %slice-start = ((s8[8388608]{0:T(1024)(128)(4,1)}), s8[4194304]{0:T(1024)(128)(4,1)S(1)}, s32[]{:S(2)}) async-start(s8[8388608]{0:T(1024)(128)(4,1)} %bitcast.5), calls=%async_computation.2 | async-start | bytes 8388608
  49.5 33.2 %slice-start.1 = ((s8[8388608]{0:T(1024)(128)(4,1)}), s8[4194304]{0:T(1024)(128)(4,1)S(1)}, s32[]{:S(2)}) async-start(s8[8388608]{0:T(1024)(128)(4,1)} %bitcast.5), calls=%async_computation.3 | async-start | bytes 8388608
